TPU v7x, 256 devices: a whole 4x4x8 slice. The times are simulated.
256 devices in a mesh: narrow: 8 (over x, core), wide: 32 (over y, z).
Axes of the slice: x: 4, y: 4, z: 8, core: 2. Of those that a mesh axis runs over, the one named last changes fastest.
Arguments:
- block_ids: int32 [4096, 4], P(('narrow', 'wide')), may hold values from 0 to 511, as said below
- incidence: int32 [4096, 4, 128, 128], P(('narrow', 'wide')), may hold values from 0 to 1
- costs: int32 [4096, 128], P(('narrow', 'wide')), may hold values from 16 to 80
- start_mult: float32 [512, 128], replicated, may hold values from 0.25 to 4
- upper: float32 [1], replicated, may hold values from 65536 to 131072
Outputs:
- multipliers: float32 [512, 128], replicated
- primal_mean: float32 [4096, 128], P(('narrow', 'wide'))
Inputs may be any that keep to these rules, and one draw needn't show every extreme that they name: `block_ids`: the 4 row blocks listed for one tile are distinct.
All inputs are finite; a program needn't handle non-finite values.
Results may differ from a plain program's by a relative error of at most 0.0003.
Values sent between devices are 32-bit elements; how exact they have to be, the bound alone decides.
No kernel may reach another device: no remote copies, remote signals or barrier semaphores. Data moves between devices by JAX's collectives and lax.ppermute only.
A program may use at most 64 MiB of HBM per device.

v0:
```python
import jax
import jax.numpy as jnp
from jax import lax
from jax.sharding import Mesh
from jax.sharding import PartitionSpec as P

BLK = 128
K = 4
ITERS = 3
NARROW_WIDE = ("narrow_0", "narrow_1", "wide_0", "wide_1")


def filled_up(lines, length):
    spare = -lines.shape[0] % length
    if not spare:
        return lines
    return jnp.concatenate([lines, jnp.zeros((spare, *lines.shape[1:]), lines.dtype)])


def sent_to_all(value, axis):
    copies = jnp.broadcast_to(value, (lax.axis_size(axis), *value.shape))
    return lax.all_to_all(copies, axis, split_axis=0, concat_axis=0, tiled=True)


def joined_along(tiles, dim):
    tiles = jnp.moveaxis(tiles, 0, dim)
    lengths = tiles.shape
    return tiles.reshape(*lengths[:dim], lengths[dim] * lengths[dim + 1], *lengths[dim + 2 :])


def gather_axes(value, axes, dim):
    far, near = axes
    tiles = sent_to_all(sent_to_all(value, far), near)
    return joined_along(tiles.swapaxes(0, 1).reshape(-1, *value.shape), dim)


def in_blocks(value, dim, length):
    lengths = value.shape
    tiles = value.reshape(*lengths[:dim], length, lengths[dim] // length, *lengths[dim + 1 :])
    return jnp.moveaxis(tiles, dim, 0)


def summed_on_arrival(value, axis, dim):
    tiles = in_blocks(value, dim, lax.axis_size(axis))
    arrived = lax.all_to_all(tiles, axis, split_axis=0, concat_axis=0, tiled=True)
    return arrived.sum(axis=0)


def sum_by_axis(value, axes, dim):
    far, near = axes
    tiles = in_blocks(value, dim, lax.axis_size(far))
    nearer = summed_on_arrival(tiles, near, dim + 1)
    arrived = lax.all_to_all(nearer, far, split_axis=0, concat_axis=0, tiled=True)
    return arrived.sum(axis=0)


def total_of(value, axes):
    padded = filled_up(value, lax.axis_size(axes[0]) * lax.axis_size(axes[1]))
    whole = gather_axes(sum_by_axis(padded, axes, 0), axes, 0)
    return lax.slice_in_dim(whole, 0, len(value)).reshape(value.shape)


def together(arrays, axis):
    vector, at, gathered = (jnp.concatenate([a.reshape(-1) for a in arrays]), 0, [])
    so_far = total_of(vector, axis)
    for a in arrays:
        gathered.append(so_far[at : at + a.size].reshape(a.shape))
        at += a.size
    return tuple(gathered)


def local(block_ids, incidence, costs, start_mult, upper):
    hi = lax.Precision.HIGHEST
    tiles_here = block_ids.shape[0]
    blocks = start_mult.shape[0]
    incf = incidence.astype(jnp.float32)
    costf = costs.astype(jnp.float32)
    onehot = (
        block_ids.reshape(tiles_here * K, 1) == jnp.arange(blocks, dtype=jnp.int32)[None, :]
    ).astype(jnp.float32)
    mult = start_mult
    primal_mean = jnp.zeros(costs.shape, jnp.float32)
    for step in range(ITERS):
        u_tile = jnp.take(mult, block_ids, axis=0)
        reduced = costf - jnp.einsum("tkrc,tkr->tc", incf, u_tile, precision=hi)
        primal = 1.0 / (1.0 + jnp.exp(reduced / 8.0))
        local_soft = jnp.sum(-8.0 * jax.nn.softplus(-reduced / 8.0))
        if step == 0:
            primal_mean = primal
        else:
            primal_mean = 0.3 * primal + 0.7 * primal_mean
        part = jnp.einsum("tkrc,tc->tkr", incf, primal_mean, precision=hi).reshape(
            tiles_here * K, BLK
        )
        row_part = jnp.dot(onehot.T, part, precision=hi, preferred_element_type=jnp.float32)
        cover, late_sum = together(
            (row_part, local_soft), (("narrow_0", "narrow_1"), ("wide_0", "wide_1"))
        )
        slope = 1.0 - cover
        norm = jnp.sum(slope * slope)
        value = jnp.sum(mult) + late_sum
        size = (upper[0] - value) / (norm + 1e-06)
        mult = jnp.maximum(0.0, mult + size * slope)
    return (mult, primal_mean)


def solution(mesh):
    split = Mesh(mesh.devices.reshape(4, 2, 4, 8), ("narrow_0", "narrow_1", "wide_0", "wide_1"))
    return jax.shard_map(
        local,
        mesh=split,
        in_specs=(
            P(NARROW_WIDE, None),
            P(NARROW_WIDE, None, None, None),
            P(NARROW_WIDE, None),
            P(),
            P(),
        ),
        out_specs=(P(), P(NARROW_WIDE, None)),
        check_vma=False,
    )
```

profile of v0, /device:TPU:1, one launch (start us, length us, event | category | flops | bytes accessed | tf_op | source)
XLA Modules:
  0.0 219.8 jit_solution(3100073725446977500)
XLA Ops:
  0.6 0.7 compare_select_fusion.3
  1.3 0.7 compare_and_fusion
  2.0 0.8 copy.31
  2.8 0.1 copy.33
  2.9 0.1 reshape.116
  3.0 0.1 copy.32
  3.1 1.5 gather_fusion
  4.6 0.1 broadcast_select_fusion.2
  4.7 4.1 %fusion.10 = f32[16,1,128,1]{2,1,3,0:T(1,128)S(1)} fusion(f32[16,4,128,1]{2,3,1,0:T(1,128)S(1)} %bitcast.92, s32[16,4,128,128]{3,2,1,0:T(8,128)} %param.8), kind=kOutput, calls=%fused_computation.16 | convolution fusion | flops 13631488 | bytes 4235264 | tf_op jit(solution)/shard_map/tkrc,tkr->tc/dot_general | solution.py:85
  8.8 0.6 fusion.16
  9.5 3.4 %fusion.8 = f32[16,1,4,128]{3,1,2,0:T(1,128)S(1)} fusion(f32[16,128,1,1]{1,2,3,0:T(1,128)S(1)} %bitcast.103, s32[16,4,128,128]{3,2,1,0:T(8,128)S(1)} %copy-done), kind=kOutput, calls=%fused_computation.14 | convolution fusion | flops 13631488 | bytes 4235264 | tf_op jit(solution)/shard_map/tkrc,tc->tkr/dot_general | solution.py:92
  12.9 0.1 eq.15
  13.0 0.5 convolution_bitcast_fusion.2
  13.4 0.9 concatenate.9
  14.3 0.4 reshape_reshape.18
  14.7 0.2 copy.34
  14.9 23.5 %all_to_all.84 = f32[32,8,257]{2,1,0:T(8,128)S(1)} all-to-all(f32[32,8,257]{2,1,0:T(8,128)S(1)} %copy.34), channel_id=1, replica_groups=mesh['narrow_0'=4,'narrow_1'=2,'wide_0'=4,'wide_1'=8] {'wide_0','wide_1'}, dimensions={0} | all-to-all | bytes 526336 | tf_op jit(solution)/shard_map/all_to_all | solution.py:45
  38.5 12.4 %all_to_all.85 = f32[8,1,257]{2,1,0:T(1,128)S(1)} all-to-all(f32[8,1,257]{2,1,0:T(1,128)S(1)} %all_to_all.55), channel_id=1, replica_groups=mesh['narrow_0'=4,'narrow_1'=2,'wide_0'=4,'wide_1'=8] {'narrow_0','narro..., dimensions={0} | all-to-all | bytes 16448 | tf_op jit(solution)/shard_map/all_to_all | solution.py:53
  51.0 7.7 %all_to_all.86 = f32[8,1,257]{2,1,0:T(1,128)S(1)} all-to-all(f32[8,1,257]{2,1,0:T(1,128)S(1)} %broadcast_in_dim.28), channel_id=1, replica_groups=mesh['narrow_0'=4,'narrow_1'=2,'wide_0'=4,'wide_1'=8] {'narrow_0','narro..., dimensions={0} | all-to-all | bytes 16448 | tf_op jit(solution)/shard_map/all_to_all | solution.py:22
  58.7 0.8 broadcast_in_dim.29
  59.5 5.1 %all-to-all-start.3 = ((f32[32,8,257]{2,1,0:T(8,128)}), f32[32,8,257]{2,1,0:T(8,128)S(1)}, u32[]{:S(2)}, u32[]{:S(2)}) async-start(f32[32,8,257]{2,1,0:T(8,128)} %broadcast_in_dim.29), calls=%async_computation.3 | async-start | bytes 786432 | tf_op jit(solution)/shard_map/all_to_all | solution.py:22
  64.6 0.7 reduce_sum.135
  65.9 10.2 %all-to-all-done.3 = f32[32,8,257]{2,1,0:T(8,128)S(1)} async-done(((f32[32,8,257]{2,1,0:T(8,128)}), f32[32,8,257]{2,1,0:T(8,128)S(1)}, u32[]{:S(2)}, u32[]{:S(2)}) %all-to-all-start.3) | async-done | bytes 263200 | tf_op jit(solution)/shard_map/all_to_all | solution.py:22
  76.2 0.4 reshape_reshape.19
  76.6 0.4 slice.37
  77.0 0.6 slice.51
  77.6 0.7 multiply_reduce_fusion.2
  80.2 0.7 fusion.22
  80.8 0.6 gather_fusion.1
  81.4 0.1 broadcast_select_fusion.1
  81.5 4.1 %fusion.6 = f32[16,1,128,1]{2,1,3,0:T(1,128)S(1)} fusion(f32[16,4,128,1]{2,3,1,0:T(1,128)S(1)} %bitcast.93, s32[16,4,128,128]{3,2,1,0:T(8,128)} %param.8), kind=kOutput, calls=%fused_computation.12 | convolution fusion | flops 13631488 | bytes 4235264 | tf_op jit(solution)/shard_map/tkrc,tkr->tc/dot_general | solution.py:85
  85.6 0.7 fusion.18
  86.3 3.4 %fusion.4 = f32[16,1,4,128]{3,1,2,0:T(1,128)S(1)} fusion(f32[16,128,1,1]{1,2,3,0:T(1,128)S(1)} %bitcast.99, s32[16,4,128,128]{3,2,1,0:T(8,128)S(1)} %copy-done.1), kind=kOutput, calls=%fused_computation.10 | convolution fusion | flops 13631488 | bytes 4235264 | tf_op jit(solution)/shard_map/tkrc,tc->tkr/dot_general | solution.py:92
  89.7 0.5 convolution_bitcast_fusion.1
  90.2 0.9 concatenate.10
  91.1 0.4 reshape_reshape.20
  91.5 0.2 copy.39
  91.8 18.0 %all_to_all.87 = f32[32,8,257]{2,1,0:T(8,128)S(1)} all-to-all(f32[32,8,257]{2,1,0:T(8,128)S(1)} %copy.39), channel_id=1, replica_groups=mesh['narrow_0'=4,'narrow_1'=2,'wide_0'=4,'wide_1'=8] {'wide_0','wide_1'}, dimensions={0} | all-to-all | bytes 526336 | tf_op jit(solution)/shard_map/all_to_all | solution.py:45
  109.8 11.6 %all_to_all.88 = f32[8,1,257]{2,1,0:T(1,128)S(1)} all-to-all(f32[8,1,257]{2,1,0:T(1,128)S(1)} %all_to_all.61), channel_id=1, replica_groups=mesh['narrow_0'=4,'narrow_1'=2,'wide_0'=4,'wide_1'=8] {'narrow_0','narro..., dimensions={0} | all-to-all | bytes 16448 | tf_op jit(solution)/shard_map/all_to_all | solution.py:53
  121.5 7.7 %all_to_all.89 = f32[8,1,257]{2,1,0:T(1,128)S(1)} all-to-all(f32[8,1,257]{2,1,0:T(1,128)S(1)} %broadcast_in_dim.30), channel_id=1, replica_groups=mesh['narrow_0'=4,'narrow_1'=2,'wide_0'=4,'wide_1'=8] {'narrow_0','narro..., dimensions={0} | all-to-all | bytes 16448 | tf_op jit(solution)/shard_map/all_to_all | solution.py:22
  129.2 16.4 %all_to_all.90 = f32[32,8,257]{2,1,0:T(8,128)S(1)} all-to-all(f32[32,8,257]{2,1,0:T(8,128)S(1)} %broadcast_in_dim.31), channel_id=1, replica_groups=mesh['narrow_0'=4,'narrow_1'=2,'wide_0'=4,'wide_1'=8] {'wide_0','wide_1'}, dimensions={0} | all-to-all | bytes 526336 | tf_op jit(solution)/shard_map/all_to_all | solution.py:22
  145.7 0.4 reshape_reshape.21
  146.1 0.4 slice.40
  146.5 0.6 slice.53
  147.1 0.7 multiply_reduce_fusion.1
  149.7 0.8 fusion.21
  150.4 0.6 gather_fusion.2
  151.0 0.1 broadcast_select_fusion
  151.1 4.1 %fusion.2 = f32[16,1,128,1]{2,1,3,0:T(1,128)S(1)} fusion(f32[16,4,128,1]{2,3,1,0:T(1,128)S(1)} %bitcast.91, s32[16,4,128,128]{3,2,1,0:T(8,128)} %param.8), kind=kOutput, calls=%fused_computation.8 | convolution fusion | flops 13631488 | bytes 4235264 | tf_op jit(solution)/shard_map/tkrc,tkr->tc/dot_general | solution.py:85
  155.2 0.6 fusion.20
  155.9 3.4 %fusion = f32[16,1,4,128]{3,1,2,0:T(1,128)S(1)} fusion(f32[16,128,1,1]{1,2,3,0:T(1,128)S(1)} %bitcast.104, s32[16,4,128,128]{3,2,1,0:T(8,128)S(1)} %copy-done.2), kind=kOutput, calls=%fused_computation.6 | convolution fusion | flops 13631488 | bytes 4235264 | tf_op jit(solution)/shard_map/tkrc,tc->tkr/dot_general | solution.py:92
  159.3 0.5 convolution_bitcast_fusion
  159.7 0.8 concatenate.11
  160.5 0.4 reshape_reshape.22
  160.9 0.2 copy.44
  161.2 18.0 %all_to_all.91 = f32[32,8,257]{2,1,0:T(8,128)S(1)} all-to-all(f32[32,8,257]{2,1,0:T(8,128)S(1)} %copy.44), channel_id=1, replica_groups=mesh['narrow_0'=4,'narrow_1'=2,'wide_0'=4,'wide_1'=8] {'wide_0','wide_1'}, dimensions={0} | all-to-all | bytes 526336 | tf_op jit(solution)/shard_map/all_to_all | solution.py:45
  179.2 11.6 %all_to_all.92 = f32[8,1,257]{2,1,0:T(1,128)S(1)} all-to-all(f32[8,1,257]{2,1,0:T(1,128)S(1)} %all_to_all.67), channel_id=1, replica_groups=mesh['narrow_0'=4,'narrow_1'=2,'wide_0'=4,'wide_1'=8] {'narrow_0','narro..., dimensions={0} | all-to-all | bytes 16448 | tf_op jit(solution)/shard_map/all_to_all | solution.py:53
  190.9 7.7 %all_to_all.93 = f32[8,1,257]{2,1,0:T(1,128)S(1)} all-to-all(f32[8,1,257]{2,1,0:T(1,128)S(1)} %broadcast_in_dim.32), channel_id=1, replica_groups=mesh['narrow_0'=4,'narrow_1'=2,'wide_0'=4,'wide_1'=8] {'narrow_0','narro..., dimensions={0} | all-to-all | bytes 16448 | tf_op jit(solution)/shard_map/all_to_all | solution.py:22
  198.6 16.4 %all_to_all.94 = f32[32,8,257]{2,1,0:T(8,128)S(1)} all-to-all(f32[32,8,257]{2,1,0:T(8,128)S(1)} %broadcast_in_dim.33), channel_id=1, replica_groups=mesh['narrow_0'=4,'narrow_1'=2,'wide_0'=4,'wide_1'=8] {'wide_0','wide_1'}, dimensions={0} | all-to-all | bytes 526336 | tf_op jit(solution)/shard_map/all_to_all | solution.py:22
  215.1 0.4 reshape_reshape.23
  215.5 0.4 slice.43
  215.9 0.5 slice.55
  216.4 0.7 multiply_reduce_fusion
  219.0 0.7 add_maximum_fusion
  (34 shorter events, 0.6 us)
Async XLA Ops:
  0.6 8.2 %copy-start.4 = (s32[16,128]{1,0:T(8,128)S(1)}, s32[16,128]{1,0:T(8,128)}, u32[]{:S(2)}) copy-start(s32[16,128]{1,0:T(8,128)} %param.9) | copy-start | bytes 24580
  4.6 4.9 %copy-start = (s32[16,4,128,128]{3,2,1,0:T(8,128)S(1)}, s32[16,4,128,128]{3,2,1,0:T(8,128)}, u32[]{:S(2)}) copy-start(s32[16,4,128,128]{3,2,1,0:T(8,128)} %param.8) | copy-start | bytes 12582916
  9.5 55.1 %copy-start.3 = (f32[512,128]{1,0:T(8,128)S(1)}, f32[512,128]{1,0:T(8,128)}, u32[]{:S(2)}) copy-start(f32[512,128]{1,0:T(8,128)} %param.10) | copy-start | bytes 786436
  59.5 16.6 %all-to-all-start.3 = ((f32[32,8,257]{2,1,0:T(8,128)}), f32[32,8,257]{2,1,0:T(8,128)S(1)}, u32[]{:S(2)}, u32[]{:S(2)}) async-start(f32[32,8,257]{2,1,0:T(8,128)} %broadcast_in_dim.29), calls=%async_computation.3 | async-start | bytes 786432 | tf_op jit(solution)/shard_map/all_to_all | solution.py:22
  81.4 4.9 %copy-start.1 = (s32[16,4,128,128]{3,2,1,0:T(8,128)S(1)}, s32[16,4,128,128]{3,2,1,0:T(8,128)}, u32[]{:S(2)}) copy-start(s32[16,4,128,128]{3,2,1,0:T(8,128)} %param.8) | copy-start | bytes 12582916
  151.0 4.8 %copy-start.2 = (s32[16,4,128,128]{3,2,1,0:T(8,128)S(1)}, s32[16,4,128,128]{3,2,1,0:T(8,128)}, u32[]{:S(2)}) copy-start(s32[16,4,128,128]{3,2,1,0:T(8,128)} %param.8) | copy-start | bytes 12582916
  155.9 59.1 %copy-start.5 = (f32[16,128]{1,0:T(8,128)}, f32[16,128]{1,0:T(8,128)S(1)}, u32[]{:S(2)}) copy-start(f32[16,128]{1,0:T(8,128)S(1)} %get-tuple-element.8) | copy-start | bytes 24580
where the time goes:
time: 223 us; the launch traced here: 220 us
  blocking collectives  151 us (68%)
  matrix products  23.9 us (11%)
  local copies, waits for them, and re-layouts  13.5 us (6%)
  waiting for transfers between devices  10.2 us (5%)
  other arithmetic  8.62 us (4%)
  between operations  7.41 us (3%)
  starting transfers between devices  5.11 us (2%)
    all_to_all x3, blocking collectives, summed_on_arrival(): lax.all_to_all(tiles, axis, split_axis=0, concat_axis=0, tiled=True)  59.5 us
    all_to_all x5, blocking collectives, sent_to_all(): return lax.all_to_all(copies, axis, split_axis=0, concat_axis=0, tiled=True)  55.9 us
    all_to_all x3, blocking collectives, sum_by_axis(): lax.all_to_all(nearer, far, split_axis=0, concat_axis=0, tiled=True)  35.6 us
    dot_general x3, matrix products, local(): reduced = costf - jnp.einsum('tkrc,tkr->tc', incf, u_tile, precision=hi)  12.3 us
    all_to_all x1, waiting for transfers between devices, sent_to_all(): return lax.all_to_all(copies, axis, split_axis=0, concat_axis=0, tiled=True)  10.2 us
    dot_general x3, matrix products, local(): jnp.einsum('tkrc,tc->tkr', incf, primal_mean, precision=hi)  10.2 us
    all_to_all x1, starting transfers between devices, sent_to_all(): return lax.all_to_all(copies, axis, split_axis=0, concat_axis=0, tiled=True)  5.11 us
  transfers between devices with their start and end apart: 1, of which 1 were waited for; matrix products, arithmetic and copies ran while one was open for 0% of the time, Pallas kernels for 0%

commit v1 on v0

v1 whole, which is shorter than its diff:
```python
import jax
import jax.numpy as jnp
from jax import lax
from jax.experimental import pallas as pl
from jax.experimental.pallas import tpu as pltpu
from jax.sharding import Mesh
from jax.sharding import PartitionSpec as P

BLK = 128
TILE = 128
K = 4
ITERS = 3
CHUNKS = 8
X, C, Y, Z = 4, 2, 4, 8
SPLIT = ("x", "c", "y", "z")
OWNERS = ("c", "x", "y")
NEAR = ("x", "y")
SLOT = 24

f32, bf16 = jnp.float32, jnp.bfloat16
VMEM = pl.BlockSpec(memory_space=pltpu.VMEM)
SMEM = pl.BlockSpec(memory_space=pltpu.SMEM)
HBM = pl.BlockSpec(memory_space=pltpu.HBM)


def three_parts(v):
    high = v.astype(bf16)
    rest = v - high.astype(f32)
    middle = rest.astype(bf16)
    return high, middle, (rest - middle.astype(f32)).astype(bf16)


def column_step(mult_ref, ids_ref, cost_ref, inc_tile, prev, rows_scr, parts_scr, mean_ref, soft_ref, cover_ref):
    tiles = cost_ref.shape[0]
    for k in range(K):
        for t in range(tiles):
            at = k * tiles + t
            rows_scr[at : at + 1, :] = mult_ref[pl.ds(ids_ref[t, k], 1), :]
    parts = three_parts(rows_scr[...])
    line = lax.broadcasted_iota(jnp.int32, (tiles, BLK), 0)
    acc = jnp.zeros((3 * tiles, TILE), f32)
    for t in range(tiles):
        keep = jnp.where(line == t, 1.0, 0.0).astype(bf16)
        lhs = jnp.concatenate(
            [
                jnp.concatenate([p[k * tiles : (k + 1) * tiles] * keep for k in range(K)], axis=1)
                for p in parts
            ],
            axis=0,
        )
        acc += jnp.dot(lhs, inc_tile(t), preferred_element_type=f32)
    priced = acc[:tiles] + acc[tiles : 2 * tiles] + acc[2 * tiles :]
    reduced = cost_ref[...].astype(f32) - priced
    scaled = reduced / 8.0
    primal = 1.0 / (1.0 + jnp.exp(scaled))
    soft = -8.0 * (jnp.maximum(-scaled, 0.0) + jnp.log1p(jnp.exp(-jnp.abs(scaled))))
    soft_ref[...] = soft[:8] + soft[8:]
    mean = primal if prev is None else 0.3 * primal + 0.7 * prev[...]
    mean_ref[...] = mean
    parts_scr[...] = jnp.zeros_like(parts_scr)
    for s, p in enumerate(three_parts(mean)):
        parts_scr[pl.ds(s, tiles, stride=8), :] = p.astype(f32)
    cover_ref[...] = jnp.zeros_like(cover_ref)
    for t in range(tiles):
        lhs = parts_scr[8 * t : 8 * (t + 1), :].astype(bf16)
        out = lax.dot_general(lhs, inc_tile(t), (((1,), (1,)), ((), ())), preferred_element_type=f32)
        part = out[0:1] + out[1:2] + out[2:3]
        for k in range(K):
            row = pl.ds(ids_ref[t, k], 1)
            cover_ref[row, :] += part[:, k * BLK : (k + 1) * BLK]


def first_kernel(ids_ref, inc_hbm, cost_ref, mult_ref, inc_ref, mean_ref, soft_ref, cover_ref, raw, rows_scr, parts_scr, sems):
    tiles = cost_ref.shape[0]
    each = tiles // CHUNKS
    copies = [
        pltpu.make_async_copy(inc_hbm.at[pl.ds(i * each, each)], raw.at[pl.ds(i * each, each)], sems.at[i])
        for i in range(CHUNKS)
    ]
    for copy in copies:
        copy.start()
    done = set()

    def inc_tile(t):
        if t not in done:
            done.add(t)
            if t % each == 0:
                copies[t // each].wait()
            inc_ref[t] = raw[t].reshape(K * BLK, TILE).astype(f32).astype(bf16)
        return inc_ref[t]

    column_step(mult_ref, ids_ref, cost_ref, inc_tile, None, rows_scr, parts_scr, mean_ref, soft_ref, cover_ref)


def row_step(own_ref, other_ref, mult_ref, upper_ref, new_ref):
    me = lax.axis_index("c")
    n, half = own_ref.shape[0], mult_ref.shape[0] // 2
    slopes, soft, norm = [], 0.0, 0.0
    for ref in (own_ref, other_ref):
        slope = 1.0 - ref[:, : SLOT - 8, :].reshape(half, BLK)
        slopes.append(slope)
        norm = norm + jnp.sum((slope * slope).reshape(half // 8, 8, BLK), axis=0)
        soft = soft + jnp.sum(ref[:, SLOT - 8 :, :], axis=0)
    total = jnp.sum(mult_ref[...].reshape(half // 4, 8, BLK), axis=0) + soft
    value = jnp.sum(total, keepdims=True)
    size = (upper_ref[0] - value) / (jnp.sum(norm, keepdims=True) + 1e-06)
    for slope, core in zip(slopes, (me, 1 - me)):
        at = pl.ds(pl.multiple_of(core * half, half), half)
        new_ref[at, :] = jnp.maximum(0.0, mult_ref[at, :] + size * slope)


def next_kernel(own_ref, other_ref, mult_ref, upper_ref, ids_ref, inc_ref, cost_ref, prev_ref, new_ref, mean_ref, soft_ref, cover_ref, rows_scr, parts_scr):
    row_step(own_ref, other_ref, mult_ref, upper_ref, new_ref)
    column_step(new_ref, ids_ref, cost_ref, lambda t: inc_ref[t], prev_ref, rows_scr, parts_scr, mean_ref, soft_ref, cover_ref)


def owner_kernel(in_ref, soft_ref, out_ref):
    total = in_ref[0]
    for i in range(1, in_ref.shape[0]):
        total += in_ref[i]
    for i in range(out_ref.shape[0]):
        out_ref[i, : SLOT - 8] = total
        out_ref[i, SLOT - 8 :] = soft_ref[...]


def spread_kernel(in_ref, out_ref):
    total = in_ref[0]
    for i in range(1, in_ref.shape[0]):
        total += in_ref[i]
    for i in range(out_ref.shape[0]):
        out_ref[i] = total


def call(kernel, name, out, specs, scratch=(), mib=8):
    return pl.pallas_call(
        kernel,
        out_shape=out,
        in_specs=specs,
        out_specs=jax.tree.map(lambda _: VMEM, out),
        scratch_shapes=scratch,
        compiler_params=pltpu.CompilerParams(vmem_limit_bytes=mib << 20),
        name=name,
    )


def local(block_ids, incidence, costs, start_mult, upper):
    tiles, rows = block_ids.shape[0], start_mult.shape[0]
    sds = jax.ShapeDtypeStruct
    columns = (sds((tiles, TILE), f32), sds((8, TILE), f32), sds((rows, BLK), f32))
    scratch = [pltpu.VMEM((tiles * K, BLK), f32), pltpu.VMEM((tiles * 8, TILE), f32)]
    inc, mean, soft, cover = call(
        first_kernel,
        "first",
        (sds((tiles, K * BLK, TILE), bf16), *columns),
        [SMEM, HBM, VMEM, VMEM],
        [pltpu.VMEM((tiles, K, BLK, TILE), jnp.int32), *scratch, pltpu.SemaphoreType.DMA((CHUNKS,))],
        mib=16,
    )(block_ids, incidence, costs, start_mult)
    mult = start_mult
    for step in range(ITERS):
        there = lax.all_to_all(cover.reshape(C * X * Y, SLOT - 8, BLK), OWNERS, 0, 0, tiled=True)
        there = call(owner_kernel, "owner", sds((Z, SLOT, BLK), f32), [VMEM] * 2)(there, soft)
        there = lax.all_to_all(there, "z", 0, 0, tiled=True)
        there = call(spread_kernel, "spread", sds((X * Y, SLOT, BLK), f32), [VMEM])(there)
        own = lax.all_to_all(there, NEAR, 0, 0, tiled=True)
        other = lax.ppermute(own, "c", [(0, 1), (1, 0)])
        if step < ITERS - 1:
            mult, mean, soft, cover = call(
                next_kernel,
                "next",
                (sds((rows, BLK), f32), *columns),
                [VMEM] * 3 + [SMEM] * 2 + [VMEM] * 3,
                scratch,
            )(own, other, mult, upper, block_ids, inc, costs, mean)
    mult = call(row_step, "last", sds((rows, BLK), f32), [VMEM] * 3 + [SMEM])(own, other, mult, upper)
    return mult, mean


def solution(mesh):
    split = Mesh(mesh.devices.reshape(X, C, Y, Z), SPLIT)
    return jax.shard_map(
        local,
        mesh=split,
        in_specs=(
            P(SPLIT, None),
            P(SPLIT, None, None, None),
            P(SPLIT, None),
            P(),
            P(),
        ),
        out_specs=(P(), P(SPLIT, None)),
        check_vma=False,
    )
```

time: 223 us -> 135 us (0.61); the launches traced: 220 us -> 135 us
  blocking collectives: 151 us -> 108 us
  matrix products: 23.9 us -> 0 us
  Pallas kernels: 0 us -> 9.06 us
  local copies, waits for them, and re-layouts: 13.5 us -> 4.59 us
  other arithmetic: 8.62 us -> 0 us
  waiting for transfers between devices: 10.2 us -> 2.56 us
  between operations: 7.41 us -> 1.33 us
  starting transfers between devices: 5.11 us -> 9.39 us
    all_to_all x11 -> x9, blocking collectives: 151 us -> 108 us  [the longest x3 42.7 us: local(): lax.all_to_all(cover.reshape(C * X * Y, SLOT - 8, BLK), OWNERS, 0, 0, til...]
    dot_general x9 -> x0, matrix products: 23.9 us -> none  [the longest x3 12.3 us: local(): reduced = costf - jnp.einsum('tkrc,tkr->tc', incf, u_tile, precision=hi)]
    all_to_all x1 -> x0, waiting for transfers between devices: 10.2 us -> none  [sent_to_all(): return lax.all_to_all(copies, axis, split_axis=0, concat_axis=0, tiled=True)]
    ppermute x0 -> x3, starting transfers between devices: none -> 9.39 us  [local(): other = lax.ppermute(own, 'c', [(0, 1), (1, 0)])]
    pallas_call x0 -> x10, Pallas kernels: none -> 9.06 us  [the longest x2 4.53 us: local(): call(next_kernel, 'next', (sds((rows, BLK), f32), *columns), [VMEM] * 3 +...]
    reduce_sum x15 -> x0, other arithmetic: 6.25 us -> none  [the longest x3 2.09 us: local(): value = jnp.sum(mult) + late_sum]
    all_to_all x1 -> x0, starting transfers between devices: 5.11 us -> none  [sent_to_all(): return lax.all_to_all(copies, axis, split_axis=0, concat_axis=0, tiled=True)]
    unnamed x16 -> x7, local copies, waits for them, and re-layouts: 0.79 us -> 4.59 us
  transfers between devices with their start and end apart: 1 -> 3, of which waited for: 1 -> 3; matrix products, arithmetic and copies ran while one was open for 0% -> 0% of each run, Pallas kernels for 0% -> 0%
where the time goes in v1:
time: 135 us
  blocking collectives  108 us (80%)
  starting transfers between devices  9.39 us (7%)
  Pallas kernels  9.06 us (7%)
  local copies, waits for them, and re-layouts  4.59 us (3%)
  waiting for transfers between devices  2.56 us (2%)
    all_to_all x3, blocking collectives, local(): lax.all_to_all(cover.reshape(C * X * Y, SLOT - 8, BLK), OWNERS, 0, 0, til...  42.7 us
    all_to_all x3, blocking collectives, local(): there = lax.all_to_all(there, 'z', 0, 0, tiled=True)  35.2 us
    all_to_all x3, blocking collectives, local(): own = lax.all_to_all(there, NEAR, 0, 0, tiled=True)  30.1 us
    ppermute x3, starting transfers between devices, local(): other = lax.ppermute(own, 'c', [(0, 1), (1, 0)])  9.39 us
    unnamed x7, local copies, waits for them, and re-layouts  4.59 us
    pallas_call x2, Pallas kernels, local(): call(next_kernel, 'next', (sds((rows, BLK), f32), *columns), [VMEM] * 3 +...  4.53 us
    pallas_call x1, Pallas kernels, local(): call(first_kernel, 'first', (sds((tiles, K * BLK, TILE), bf16), *columns)...  3.41 us
  transfers between devices with their start and end apart: 3, of which 3 were waited for; matrix products, arithmetic and copies ran while one was open for 0% of the time, Pallas kernels for 0%

profile of v1, /device:TPU:1, one launch (start us, length us, event | category | flops | bytes accessed | tf_op | source)
XLA Modules:
  0.0 134.9 jit_solution(11999220397889945807)
XLA Ops:
  0.6 0.8 copy.7.ids_ref
  1.4 0.0 copy-start
  1.4 2.2 %copy-done = s32[16,4,128,128]{3,2,1,0:T(8,128)S(1)} copy-done((s32[16,4,128,128]{3,2,1,0:T(8,128)S(1)}, s32[16,4,128,128]{3,2,1,0:T(8,128)}, u32[]{:S(2)}) %copy-start) | copy-done | bytes 4194328
  3.6 0.0 copy-start.1
  3.6 0.9 copy-done.1
  4.5 0.0 copy-start.2
  4.5 0.7 copy-done.2
  5.2 3.4 %first.1 = (bf16[16,512,128]{2,1,0:T(8,128)(2,1)S(1)}, f32[16,128]{1,0:T(8,128)S(1)}, f32[8,128]{1,0:T(8,128)S(1)}, f32[512,128]{1,0:T(8,128)S(1)}) custom-call(s32[16,4]{1,0:T(8,128)S(1)} %copy.7.ids_ref, s32[16,4,128,128]{3,2,1,0:T(8,128)S(1)} %copy-done, s32[16,128]{1,0:T(8,128)S(1)} %copy-done.2, f32[512,128]{1,0:T(8,128)S(1)} %copy-done.1), custom_call_target="tpu_custom_call" | custom-call | tf_op jit(solution)/shard_map/first/pallas_call | solution.py:151
  8.6 17.2 %all_to_all.45.in_ref = f32[32,16,128]{2,1,0:T(8,128)S(1)} all-to-all(f32[32,16,128]{2,1,0:T(8,128)S(1)} %bitcast.5), channel_id=1, replica_groups=mesh['x'=4,'c'=2,'y'=4,'z'=8] {'c','x','y'}, dimensions={0} | all-to-all | bytes 524288 | tf_op jit(solution)/shard_map/all_to_all | solution.py:161
  25.9 15.6 %all_to_all.46.in_ref = f32[8,24,128]{2,1,0:T(8,128)S(1)} all-to-all(f32[8,24,128]{2,1,0:T(8,128)S(1)} %owner.3), channel_id=1, replica_groups=mesh['x'=4,'c'=2,'y'=4,'z'=8] {'z'}, dimensions={0} | all-to-all | bytes 196608 | tf_op jit(solution)/shard_map/all_to_all | solution.py:163
  41.5 9.9 %all_to_all.47.own_ref = f32[16,24,128]{2,1,0:T(8,128)S(1)} all-to-all(f32[16,24,128]{2,1,0:T(8,128)S(1)} %spread.3), channel_id=1, replica_groups=mesh['x'=4,'c'=2,'y'=4,'z'=8] {'x','y'}, dimensions={0} | all-to-all | bytes 393216 | tf_op jit(solution)/shard_map/all_to_all | solution.py:165
  51.4 3.2 %collective-permute-start = (f32[16,24,128]{2,1,0:T(8,128)S(1)}, f32[16,24,128]{2,1,0:T(8,128)S(1)}, u32[]{:S(2)}, u32[]{:S(2)}) collective-permute-start(f32[16,24,128]{2,1,0:T(8,128)S(1)} %all_to_all.47.own_ref), channel_id=1, source_target_pairs={{0,32},{32,0},{1,33},{33,1},{2,34},{34,2},{3,35},{35,3},{4,36},{36... | collective-permute-start | bytes 589832 | tf_op jit(solution)/shard_map/ppermute | solution.py:166
  55.3 0.4 collective-permute-done.other_ref
  55.7 2.0 %next.2 = (f32[512,128]{1,0:T(8,128)S(1)}, f32[16,128]{1,0:T(8,128)S(1)}, f32[8,128]{1,0:T(8,128)S(1)}, f32[512,128]{1,0:T(8,128)S(1)}) custom-call(f32[16,24,128]{2,1,0:T(8,128)S(1)} %all_to_all.47.own_ref, f32[16,24,128]{2,1,0:T(8,128)S(1)} %collective-permute-done.other_ref, f32[512,128]{1,0:T(8,128)S(1)} %copy-done.1, f32[1]{0:T(128)S(6)} %copy.10.upper_ref, ...), custom_call_target="tpu_custom_call" | custom-call | tf_op jit(solution)/shard_map/next/pallas_call | solution.py:168
  57.7 12.8 %all_to_all.48.in_ref = f32[32,16,128]{2,1,0:T(8,128)S(1)} all-to-all(f32[32,16,128]{2,1,0:T(8,128)S(1)} %bitcast.4), channel_id=1, replica_groups=mesh['x'=4,'c'=2,'y'=4,'z'=8] {'c','x','y'}, dimensions={0} | all-to-all | bytes 524288 | tf_op jit(solution)/shard_map/all_to_all | solution.py:161
  70.5 9.8 %all_to_all.49.in_ref = f32[8,24,128]{2,1,0:T(8,128)S(1)} all-to-all(f32[8,24,128]{2,1,0:T(8,128)S(1)} %owner.4), channel_id=1, replica_groups=mesh['x'=4,'c'=2,'y'=4,'z'=8] {'z'}, dimensions={0} | all-to-all | bytes 196608 | tf_op jit(solution)/shard_map/all_to_all | solution.py:163
  80.4 10.1 %all_to_all.50.own_ref = f32[16,24,128]{2,1,0:T(8,128)S(1)} all-to-all(f32[16,24,128]{2,1,0:T(8,128)S(1)} %spread.4), channel_id=1, replica_groups=mesh['x'=4,'c'=2,'y'=4,'z'=8] {'x','y'}, dimensions={0} | all-to-all | bytes 393216 | tf_op jit(solution)/shard_map/all_to_all | solution.py:165
  90.5 3.1 %collective-permute-start.1 = (f32[16,24,128]{2,1,0:T(8,128)S(1)}, f32[16,24,128]{2,1,0:T(8,128)S(1)}, u32[]{:S(2)}, u32[]{:S(2)}) collective-permute-start(f32[16,24,128]{2,1,0:T(8,128)S(1)} %all_to_all.50.own_ref), channel_id=1, source_target_pairs={{0,32},{32,0},{1,33},{33,1},{2,34},{34,2},{3,35},{35,3},{4,36},{36... | collective-permute-start | bytes 589832 | tf_op jit(solution)/shard_map/ppermute | solution.py:166
  93.5 1.1 collective-permute-done.1.other_ref
  94.6 2.5 %next.3 = (f32[512,128]{1,0:T(8,128)S(1)}, f32[16,128]{1,0:T(8,128)}, f32[8,128]{1,0:T(8,128)S(1)}, f32[512,128]{1,0:T(8,128)S(1)}) custom-call(f32[16,24,128]{2,1,0:T(8,128)S(1)} %all_to_all.50.own_ref, f32[16,24,128]{2,1,0:T(8,128)S(1)} %collective-permute-done.1.other_ref, f32[512,128]{1,0:T(8,128)S(1)} %get-tuple-element.20.mult_ref, ...), custom_call_target="tpu_custom_call" | custom-call | tf_op jit(solution)/shard_map/next/pallas_call | solution.py:168
  97.1 12.7 %all_to_all.51.in_ref = f32[32,16,128]{2,1,0:T(8,128)S(1)} all-to-all(f32[32,16,128]{2,1,0:T(8,128)S(1)} %bitcast.3), channel_id=1, replica_groups=mesh['x'=4,'c'=2,'y'=4,'z'=8] {'c','x','y'}, dimensions={0} | all-to-all | bytes 524288 | tf_op jit(solution)/shard_map/all_to_all | solution.py:161
  109.9 9.8 %all_to_all.52.in_ref = f32[8,24,128]{2,1,0:T(8,128)S(1)} all-to-all(f32[8,24,128]{2,1,0:T(8,128)S(1)} %owner.5), channel_id=1, replica_groups=mesh['x'=4,'c'=2,'y'=4,'z'=8] {'z'}, dimensions={0} | all-to-all | bytes 196608 | tf_op jit(solution)/shard_map/all_to_all | solution.py:163
  119.8 10.1 %all_to_all.53.own_ref = f32[16,24,128]{2,1,0:T(8,128)S(1)} all-to-all(f32[16,24,128]{2,1,0:T(8,128)S(1)} %spread.5), channel_id=1, replica_groups=mesh['x'=4,'c'=2,'y'=4,'z'=8] {'x','y'}, dimensions={0} | all-to-all | bytes 393216 | tf_op jit(solution)/shard_map/all_to_all | solution.py:165
  129.8 3.1 %collective-permute-start.2 = (f32[16,24,128]{2,1,0:T(8,128)S(1)}, f32[16,24,128]{2,1,0:T(8,128)S(1)}, u32[]{:S(2)}, u32[]{:S(2)}) collective-permute-start(f32[16,24,128]{2,1,0:T(8,128)S(1)} %all_to_all.53.own_ref), channel_id=1, source_target_pairs={{0,32},{32,0},{1,33},{33,1},{2,34},{34,2},{3,35},{35,3},{4,36},{36... | collective-permute-start | bytes 589832 | tf_op jit(solution)/shard_map/ppermute | solution.py:166
  132.9 1.1 collective-permute-done.2.other_ref
  134.0 0.9 last.1
  (6 shorter events, 0.2 us)
Async XLA Ops:
  1.4 2.2 %copy-start = (s32[16,4,128,128]{3,2,1,0:T(8,128)S(1)}, s32[16,4,128,128]{3,2,1,0:T(8,128)}, u32[]{:S(2)}) copy-start(s32[16,4,128,128]{3,2,1,0:T(8,128)} %inc_hbm.1) | copy-start | bytes 12582916
  3.6 0.9 copy-start.1
  4.5 0.7 copy-start.2
  51.4 4.3 %collective-permute-start = (f32[16,24,128]{2,1,0:T(8,128)S(1)}, f32[16,24,128]{2,1,0:T(8,128)S(1)}, u32[]{:S(2)}, u32[]{:S(2)}) collective-permute-start(f32[16,24,128]{2,1,0:T(8,128)S(1)} %all_to_all.47.own_ref), channel_id=1, source_target_pairs={{0,32},{32,0},{1,33},{33,1},{2,34},{34,2},{3,35},{35,3},{4,36},{36... | collective-permute-start | bytes 589832 | tf_op jit(solution)/shard_map/ppermute | solution.py:166
  90.5 4.2 %collective-permute-start.1 = (f32[16,24,128]{2,1,0:T(8,128)S(1)}, f32[16,24,128]{2,1,0:T(8,128)S(1)}, u32[]{:S(2)}, u32[]{:S(2)}) collective-permute-start(f32[16,24,128]{2,1,0:T(8,128)S(1)} %all_to_all.50.own_ref), channel_id=1, source_target_pairs={{0,32},{32,0},{1,33},{33,1},{2,34},{34,2},{3,35},{35,3},{4,36},{36... | collective-permute-start | bytes 589832 | tf_op jit(solution)/shard_map/ppermute | solution.py:166
  129.8 4.2 %collective-permute-start.2 = (f32[16,24,128]{2,1,0:T(8,128)S(1)}, f32[16,24,128]{2,1,0:T(8,128)S(1)}, u32[]{:S(2)}, u32[]{:S(2)}) collective-permute-start(f32[16,24,128]{2,1,0:T(8,128)S(1)} %all_to_all.53.own_ref), channel_id=1, source_target_pairs={{0,32},{32,0},{1,33},{33,1},{2,34},{34,2},{3,35},{35,3},{4,36},{36... | collective-permute-start | bytes 589832 | tf_op jit(solution)/shard_map/ppermute | solution.py:166

commit v2 on v1

--- a/solution.py
+++ b/solution.py
@@ -24,72 +24,87 @@
 
 
 def three_parts(v):
-    high = v.astype(bf16)
-    rest = v - high.astype(f32)
-    middle = rest.astype(bf16)
-    return high, middle, (rest - middle.astype(f32)).astype(bf16)
+    high = v.astype(bf16).astype(f32)
+    rest = v - high
+    middle = rest.astype(bf16).astype(f32)
+    return high, middle, rest - middle
 
 
 def column_step(mult_ref, ids_ref, cost_ref, inc_tile, prev, rows_scr, parts_scr, mean_ref, soft_ref, cover_ref):
     tiles = cost_ref.shape[0]
-    for k in range(K):
-        for t in range(tiles):
-            at = k * tiles + t
-            rows_scr[at : at + 1, :] = mult_ref[pl.ds(ids_ref[t, k], 1), :]
-    parts = three_parts(rows_scr[...])
-    line = lax.broadcasted_iota(jnp.int32, (tiles, BLK), 0)
-    acc = jnp.zeros((3 * tiles, TILE), f32)
     for t in range(tiles):
-        keep = jnp.where(line == t, 1.0, 0.0).astype(bf16)
-        lhs = jnp.concatenate(
-            [
-                jnp.concatenate([p[k * tiles : (k + 1) * tiles] * keep for k in range(K)], axis=1)
-                for p in parts
-            ],
-            axis=0,
+        for k in range(K):
+            at = (t // 8 * K + k) * 8 + t % 8
+            rows_scr[at : at + 1, :] = mult_ref[pl.ds(ids_ref[k, t], 1), :]
+    parts_scr[...] = jnp.zeros_like(parts_scr)
+    cover_ref[...] = jnp.zeros_like(cover_ref)
+    line = lax.broadcasted_iota(jnp.int32, (8, BLK), 0)
+    none = jnp.zeros((8, BLK), f32)
+    soft_sum = none
+    for group in range(tiles // 8):
+        first = group * 8
+        parts = [
+            three_parts(rows_scr[(group * K + k) * 8 : (group * K + k + 1) * 8, :]) for k in range(K)
+        ]
+        acc = jnp.zeros((32, TILE), f32)
+        for t in range(8):
+            lhs = [
+                jnp.concatenate([jnp.where(line == t, p, 0.0) for p in parts[k]] + [none], axis=0)
+                for k in range(K)
+            ]
+            lhs = jnp.concatenate(lhs, axis=1).astype(bf16)
+            acc += jnp.dot(lhs, inc_tile(first + t), preferred_element_type=f32)
+        here = slice(first, first + 8)
+        reduced = cost_ref[here, :].astype(f32) - (acc[:8] + acc[8:16] + acc[16:24])
+        scaled = reduced / 8.0
+        primal = 1.0 / (1.0 + jnp.exp(scaled))
+        soft_sum += -8.0 * (jnp.maximum(-scaled, 0.0) + jnp.log1p(jnp.exp(-jnp.abs(scaled))))
+        mean = primal if prev is None else 0.3 * primal + 0.7 * prev[here, :]
+        mean_ref[here, :] = mean
+        for s, p in enumerate(three_parts(mean)):
+            parts_scr[pl.ds(first * 8 + s, 8, stride=8), :] = p
+        for t in range(first, first + 8):
+            lhs = parts_scr[8 * t : 8 * (t + 1), :].astype(bf16)
+            out = lax.dot_general(
+                lhs, inc_tile(t), (((1,), (1,)), ((), ())), preferred_element_type=f32
+            )
+            part = out[0:1] + out[1:2] + out[2:3]
+            for k in range(K):
+                cover_ref[pl.ds(ids_ref[k, t], 1), :] += part[:, k * BLK : (k + 1) * BLK]
+    soft_ref[...] = soft_sum
+
+
+def first_kernel(
+    ids_hbm, inc_hbm, cost_hbm, mult_hbm, inc_ref, mean_ref, soft_ref, cover_ref,
+    ids, raw, cost, mult, rows_scr, parts_scr, sems,
+):
+    tiles = cost.shape[0]
+    each = tiles // CHUNKS
+    small = [
+        pltpu.make_async_copy(src, dst, sems.at[CHUNKS + i])
+        for i, (src, dst) in enumerate(((ids_hbm, ids), (mult_hbm, mult), (cost_hbm, cost)))
+    ]
+    chunks = [
+        pltpu.make_async_copy(
+            inc_hbm.at[pl.ds(i * each, each)], raw.at[pl.ds(i * each, each)], sems.at[i]
         )
-        acc += jnp.dot(lhs, inc_tile(t), preferred_element_type=f32)
-    priced = acc[:tiles] + acc[tiles : 2 * tiles] + acc[2 * tiles :]
-    reduced = cost_ref[...].astype(f32) - priced
-    scaled = reduced / 8.0
-    primal = 1.0 / (1.0 + jnp.exp(scaled))
-    soft = -8.0 * (jnp.maximum(-scaled, 0.0) + jnp.log1p(jnp.exp(-jnp.abs(scaled))))
-    soft_ref[...] = soft[:8] + soft[8:]
-    mean = primal if prev is None else 0.3 * primal + 0.7 * prev[...]
-    mean_ref[...] = mean
-    parts_scr[...] = jnp.zeros_like(parts_scr)
-    for s, p in enumerate(three_parts(mean)):
-        parts_scr[pl.ds(s, tiles, stride=8), :] = p.astype(f32)
-    cover_ref[...] = jnp.zeros_like(cover_ref)
-    for t in range(tiles):
-        lhs = parts_scr[8 * t : 8 * (t + 1), :].astype(bf16)
-        out = lax.dot_general(lhs, inc_tile(t), (((1,), (1,)), ((), ())), preferred_element_type=f32)
-        part = out[0:1] + out[1:2] + out[2:3]
-        for k in range(K):
-            row = pl.ds(ids_ref[t, k], 1)
-            cover_ref[row, :] += part[:, k * BLK : (k + 1) * BLK]
-
-
-def first_kernel(ids_ref, inc_hbm, cost_ref, mult_ref, inc_ref, mean_ref, soft_ref, cover_ref, raw, rows_scr, parts_scr, sems):
-    tiles = cost_ref.shape[0]
-    each = tiles // CHUNKS
-    copies = [
-        pltpu.make_async_copy(inc_hbm.at[pl.ds(i * each, each)], raw.at[pl.ds(i * each, each)], sems.at[i])
         for i in range(CHUNKS)
     ]
-    for copy in copies:
+    for copy in small + chunks:
         copy.start()
-    done = set()
+    for copy in small:
+        copy.wait()
+    seen = set()
 
     def inc_tile(t):
-        if t not in done:
-            done.add(t)
+        if t not in seen:
+            seen.add(t)
             if t % each == 0:
-                copies[t // each].wait()
+                chunks[t // each].wait()
             inc_ref[t] = raw[t].reshape(K * BLK, TILE).astype(f32).astype(bf16)
         return inc_ref[t]
 
-    column_step(mult_ref, ids_ref, cost_ref, inc_tile, None, rows_scr, parts_scr, mean_ref, soft_ref, cover_ref)
+    column_step(mult, ids, cost, inc_tile, None, rows_scr, parts_scr, mean_ref, soft_ref, cover_ref)
 
 
 def row_step(own_ref, other_ref, mult_ref, upper_ref, new_ref):
@@ -146,16 +161,24 @@
 def local(block_ids, incidence, costs, start_mult, upper):
     tiles, rows = block_ids.shape[0], start_mult.shape[0]
     sds = jax.ShapeDtypeStruct
+    ids = block_ids.T
     columns = (sds((tiles, TILE), f32), sds((8, TILE), f32), sds((rows, BLK), f32))
     scratch = [pltpu.VMEM((tiles * K, BLK), f32), pltpu.VMEM((tiles * 8, TILE), f32)]
     inc, mean, soft, cover = call(
         first_kernel,
         "first",
         (sds((tiles, K * BLK, TILE), bf16), *columns),
-        [SMEM, HBM, VMEM, VMEM],
-        [pltpu.VMEM((tiles, K, BLK, TILE), jnp.int32), *scratch, pltpu.SemaphoreType.DMA((CHUNKS,))],
+        [HBM] * 4,
+        [
+            pltpu.SMEM((K, tiles), jnp.int32),
+            pltpu.VMEM((tiles, K, BLK, TILE), jnp.int32),
+            pltpu.VMEM((tiles, TILE), jnp.int32),
+            pltpu.VMEM((rows, BLK), f32),
+            *scratch,
+            pltpu.SemaphoreType.DMA((CHUNKS + 3,)),
+        ],
         mib=16,
-    )(block_ids, incidence, costs, start_mult)
+    )(*(pltpu.with_memory_space_constraint(a, pltpu.HBM) for a in (ids, incidence, costs, start_mult)))
     mult = start_mult
     for step in range(ITERS):
         there = lax.all_to_all(cover.reshape(C * X * Y, SLOT - 8, BLK), OWNERS, 0, 0, tiled=True)
@@ -171,7 +194,7 @@
                 (sds((rows, BLK), f32), *columns),
                 [VMEM] * 3 + [SMEM] * 2 + [VMEM] * 3,
                 scratch,
-            )(own, other, mult, upper, block_ids, inc, costs, mean)
+            )(own, other, mult, upper, ids, inc, costs, mean)
     mult = call(row_step, "last", sds((rows, BLK), f32), [VMEM] * 3 + [SMEM])(own, other, mult, upper)
     return mult, mean
 

time: 135 us -> 131 us (0.970)
  local copies, waits for them, and re-layouts: 4.59 us -> 0.01 us
    unnamed x7 -> x6, local copies, waits for them, and re-layouts: 4.59 us -> 0.01 us
where the time goes in v2:
time: 131 us
  blocking collectives  108 us (82%)
  starting transfers between devices  9.39 us (7%)
  Pallas kernels  9.24 us (7%)
  waiting for transfers between devices  2.56 us (2%)
  between operations  1.35 us (1%)
    all_to_all x3, blocking collectives, local(): lax.all_to_all(cover.reshape(C * X * Y, SLOT - 8, BLK), OWNERS, 0, 0, til...  42.7 us
    all_to_all x3, blocking collectives, local(): there = lax.all_to_all(there, 'z', 0, 0, tiled=True)  35.2 us
    all_to_all x3, blocking collectives, local(): own = lax.all_to_all(there, NEAR, 0, 0, tiled=True)  30.1 us
    ppermute x3, starting transfers between devices, local(): other = lax.ppermute(own, 'c', [(0, 1), (1, 0)])  9.39 us
    pallas_call x2, Pallas kernels, local(): call(next_kernel, 'next', (sds((rows, BLK), f32), *columns), [VMEM] * 3 +...  4.51 us
    pallas_call x1, Pallas kernels, local(): call(first_kernel, 'first', (sds((tiles, K * BLK, TILE), bf16), *columns)...  3.62 us
  transfers between devices with their start and end apart: 3, of which 3 were waited for; matrix products, arithmetic and copies ran while one was open for 0% of the time, Pallas kernels for 0%

profile of v2, /device:TPU:1, one launch (start us, length us, event | category | flops | bytes accessed | tf_op | source)
XLA Modules:
  0.0 130.6 jit_solution(9168632259215019788)
XLA Ops:
  0.6 0.0 copy-start.1
  0.6 0.0 copy-start
  0.7 0.0 copy-start.2
  0.7 3.6 %first.1 = (bf16[16,512,128]{2,1,0:T(8,128)(2,1)S(1)}, f32[16,128]{1,0:T(8,128)S(1)}, f32[8,128]{1,0:T(8,128)S(1)}, f32[512,128]{1,0:T(8,128)S(1)}) custom-call(s32[4,16]{1,0:T(4,128)} %bitcast.7, s32[16,4,128,128]{3,2,1,0:T(8,128)} %inc_hbm.1, s32[16,128]{1,0:T(8,128)} %cost_ref.3, f32[512,128]{1,0:T(8,128)} %mult_ref.1), custom_call_target="tpu_custom_call" | custom-call | tf_op jit(solution)/shard_map/first/pallas_call | solution.py:167
  4.3 17.2 %all_to_all.45.in_ref = f32[32,16,128]{2,1,0:T(8,128)S(1)} all-to-all(f32[32,16,128]{2,1,0:T(8,128)S(1)} %bitcast.6), channel_id=1, replica_groups=mesh['x'=4,'c'=2,'y'=4,'z'=8] {'c','x','y'}, dimensions={0} | all-to-all | bytes 524288 | tf_op jit(solution)/shard_map/all_to_all | solution.py:184
  21.5 15.6 %all_to_all.46.in_ref = f32[8,24,128]{2,1,0:T(8,128)S(1)} all-to-all(f32[8,24,128]{2,1,0:T(8,128)S(1)} %owner.3), channel_id=1, replica_groups=mesh['x'=4,'c'=2,'y'=4,'z'=8] {'z'}, dimensions={0} | all-to-all | bytes 196608 | tf_op jit(solution)/shard_map/all_to_all | solution.py:186
  37.1 9.9 %all_to_all.47.own_ref = f32[16,24,128]{2,1,0:T(8,128)S(1)} all-to-all(f32[16,24,128]{2,1,0:T(8,128)S(1)} %spread.3), channel_id=1, replica_groups=mesh['x'=4,'c'=2,'y'=4,'z'=8] {'x','y'}, dimensions={0} | all-to-all | bytes 393216 | tf_op jit(solution)/shard_map/all_to_all | solution.py:188
  47.0 3.2 %collective-permute-start = (f32[16,24,128]{2,1,0:T(8,128)S(1)}, f32[16,24,128]{2,1,0:T(8,128)S(1)}, u32[]{:S(2)}, u32[]{:S(2)}) collective-permute-start(f32[16,24,128]{2,1,0:T(8,128)S(1)} %all_to_all.47.own_ref), channel_id=1, source_target_pairs={{0,32},{32,0},{1,33},{33,1},{2,34},{34,2},{3,35},{35,3},{4,36},{36... | collective-permute-start | bytes 589832 | tf_op jit(solution)/shard_map/ppermute | solution.py:189
  50.9 0.4 collective-permute-done.other_ref
  51.3 0.0 copy-done.1
  51.4 0.0 copy-done
  51.4 0.0 copy-done.2
  51.4 2.0 %next.2 = (f32[512,128]{1,0:T(8,128)S(1)}, f32[16,128]{1,0:T(8,128)S(1)}, f32[8,128]{1,0:T(8,128)S(1)}, f32[512,128]{1,0:T(8,128)S(1)}) custom-call(f32[16,24,128]{2,1,0:T(8,128)S(1)} %all_to_all.47.own_ref, f32[16,24,128]{2,1,0:T(8,128)S(1)} %collective-permute-done.other_ref, f32[512,128]{1,0:T(8,128)S(1)} %copy-done, f32[1]{0:T(128)S(6)} %copy.7.upper_ref, ...), custom_call_target="tpu_custom_call" | custom-call | tf_op jit(solution)/shard_map/next/pallas_call | solution.py:191
  53.4 12.8 %all_to_all.48.in_ref = f32[32,16,128]{2,1,0:T(8,128)S(1)} all-to-all(f32[32,16,128]{2,1,0:T(8,128)S(1)} %bitcast.5), channel_id=1, replica_groups=mesh['x'=4,'c'=2,'y'=4,'z'=8] {'c','x','y'}, dimensions={0} | all-to-all | bytes 524288 | tf_op jit(solution)/shard_map/all_to_all | solution.py:184
  66.2 9.8 %all_to_all.49.in_ref = f32[8,24,128]{2,1,0:T(8,128)S(1)} all-to-all(f32[8,24,128]{2,1,0:T(8,128)S(1)} %owner.4), channel_id=1, replica_groups=mesh['x'=4,'c'=2,'y'=4,'z'=8] {'z'}, dimensions={0} | all-to-all | bytes 196608 | tf_op jit(solution)/shard_map/all_to_all | solution.py:186
  76.0 10.1 %all_to_all.50.own_ref = f32[16,24,128]{2,1,0:T(8,128)S(1)} all-to-all(f32[16,24,128]{2,1,0:T(8,128)S(1)} %spread.4), channel_id=1, replica_groups=mesh['x'=4,'c'=2,'y'=4,'z'=8] {'x','y'}, dimensions={0} | all-to-all | bytes 393216 | tf_op jit(solution)/shard_map/all_to_all | solution.py:188
  86.1 3.1 %collective-permute-start.1 = (f32[16,24,128]{2,1,0:T(8,128)S(1)}, f32[16,24,128]{2,1,0:T(8,128)S(1)}, u32[]{:S(2)}, u32[]{:S(2)}) collective-permute-start(f32[16,24,128]{2,1,0:T(8,128)S(1)} %all_to_all.50.own_ref), channel_id=1, source_target_pairs={{0,32},{32,0},{1,33},{33,1},{2,34},{34,2},{3,35},{35,3},{4,36},{36... | collective-permute-start | bytes 589832 | tf_op jit(solution)/shard_map/ppermute | solution.py:189
  89.2 1.1 collective-permute-done.1.other_ref
  90.3 2.5 %next.3 = (f32[512,128]{1,0:T(8,128)S(1)}, f32[16,128]{1,0:T(8,128)}, f32[8,128]{1,0:T(8,128)S(1)}, f32[512,128]{1,0:T(8,128)S(1)}) custom-call(f32[16,24,128]{2,1,0:T(8,128)S(1)} %all_to_all.50.own_ref, f32[16,24,128]{2,1,0:T(8,128)S(1)} %collective-permute-done.1.other_ref, f32[512,128]{1,0:T(8,128)S(1)} %get-tuple-element.20.mult_ref, ...), custom_call_target="tpu_custom_call" | custom-call | tf_op jit(solution)/shard_map/next/pallas_call | solution.py:191
  92.8 12.8 %all_to_all.51.in_ref = f32[32,16,128]{2,1,0:T(8,128)S(1)} all-to-all(f32[32,16,128]{2,1,0:T(8,128)S(1)} %bitcast.4), channel_id=1, replica_groups=mesh['x'=4,'c'=2,'y'=4,'z'=8] {'c','x','y'}, dimensions={0} | all-to-all | bytes 524288 | tf_op jit(solution)/shard_map/all_to_all | solution.py:184
  105.6 9.8 %all_to_all.52.in_ref = f32[8,24,128]{2,1,0:T(8,128)S(1)} all-to-all(f32[8,24,128]{2,1,0:T(8,128)S(1)} %owner.5), channel_id=1, replica_groups=mesh['x'=4,'c'=2,'y'=4,'z'=8] {'z'}, dimensions={0} | all-to-all | bytes 196608 | tf_op jit(solution)/shard_map/all_to_all | solution.py:186
  115.4 10.1 %all_to_all.53.own_ref = f32[16,24,128]{2,1,0:T(8,128)S(1)} all-to-all(f32[16,24,128]{2,1,0:T(8,128)S(1)} %spread.5), channel_id=1, replica_groups=mesh['x'=4,'c'=2,'y'=4,'z'=8] {'x','y'}, dimensions={0} | all-to-all | bytes 393216 | tf_op jit(solution)/shard_map/all_to_all | solution.py:188
  125.5 3.1 %collective-permute-start.2 = (f32[16,24,128]{2,1,0:T(8,128)S(1)}, f32[16,24,128]{2,1,0:T(8,128)S(1)}, u32[]{:S(2)}, u32[]{:S(2)}) collective-permute-start(f32[16,24,128]{2,1,0:T(8,128)S(1)} %all_to_all.53.own_ref), channel_id=1, source_target_pairs={{0,32},{32,0},{1,33},{33,1},{2,34},{34,2},{3,35},{35,3},{4,36},{36... | collective-permute-start | bytes 589832 | tf_op jit(solution)/shard_map/ppermute | solution.py:189
  128.6 1.1 collective-permute-done.2.other_ref
  129.6 0.9 last.1
  (6 shorter events, 0.2 us)
Async XLA Ops:
  0.6 50.7 %copy-start.1 = (s32[16,128]{1,0:T(8,128)S(1)}, s32[16,128]{1,0:T(8,128)}, u32[]{:S(2)}) copy-start(s32[16,128]{1,0:T(8,128)} %cost_ref.3) | copy-start | bytes 24580
  0.6 50.7 %copy-start = (f32[512,128]{1,0:T(8,128)S(1)}, f32[512,128]{1,0:T(8,128)}, u32[]{:S(2)}) copy-start(f32[512,128]{1,0:T(8,128)} %mult_ref.1) | copy-start | bytes 786436
  0.7 50.7 %copy-start.2 = (s32[16,4]{0,1:T(4,128)S(1)}, s32[16,4]{0,1:T(4,128)}, u32[]{:S(2)}) copy-start(s32[16,4]{0,1:T(4,128)} %param.5) | copy-start | bytes 772
  47.0 4.3 %collective-permute-start = (f32[16,24,128]{2,1,0:T(8,128)S(1)}, f32[16,24,128]{2,1,0:T(8,128)S(1)}, u32[]{:S(2)}, u32[]{:S(2)}) collective-permute-start(f32[16,24,128]{2,1,0:T(8,128)S(1)} %all_to_all.47.own_ref), channel_id=1, source_target_pairs={{0,32},{32,0},{1,33},{33,1},{2,34},{34,2},{3,35},{35,3},{4,36},{36... | collective-permute-start | bytes 589832 | tf_op jit(solution)/shard_map/ppermute | solution.py:189
  86.1 4.2 %collective-permute-start.1 = (f32[16,24,128]{2,1,0:T(8,128)S(1)}, f32[16,24,128]{2,1,0:T(8,128)S(1)}, u32[]{:S(2)}, u32[]{:S(2)}) collective-permute-start(f32[16,24,128]{2,1,0:T(8,128)S(1)} %all_to_all.50.own_ref), channel_id=1, source_target_pairs={{0,32},{32,0},{1,33},{33,1},{2,34},{34,2},{3,35},{35,3},{4,36},{36... | collective-permute-start | bytes 589832 | tf_op jit(solution)/shard_map/ppermute | solution.py:189
  125.5 4.2 %collective-permute-start.2 = (f32[16,24,128]{2,1,0:T(8,128)S(1)}, f32[16,24,128]{2,1,0:T(8,128)S(1)}, u32[]{:S(2)}, u32[]{:S(2)}) collective-permute-start(f32[16,24,128]{2,1,0:T(8,128)S(1)} %all_to_all.53.own_ref), channel_id=1, source_target_pairs={{0,32},{32,0},{1,33},{33,1},{2,34},{34,2},{3,35},{35,3},{4,36},{36... | collective-permute-start | bytes 589832 | tf_op jit(solution)/shard_map/ppermute | solution.py:189

commit v3 on v2

v3 whole, which is shorter than its diff:
```python
import jax
import jax.numpy as jnp
from jax import lax
from jax.experimental import pallas as pl
from jax.experimental.pallas import tpu as pltpu
from jax.sharding import Mesh
from jax.sharding import PartitionSpec as P

BLK = 128
TILE = 128
K = 4
ITERS = 3
X, C, Y, Z = 4, 2, 4, 8
SPLIT = ("x", "c", "y", "z")
OWNERS = ("c", "x", "y")
NEAR = ("x", "y")
SLOT = 24

f32, bf16 = jnp.float32, jnp.bfloat16
INC = bf16
VMEM = pl.BlockSpec(memory_space=pltpu.VMEM)
SMEM = pl.BlockSpec(memory_space=pltpu.SMEM)
HBM = pl.BlockSpec(memory_space=pltpu.HBM)


def three_parts(v):
    high = v.astype(bf16).astype(f32)
    rest = v - high
    middle = rest.astype(bf16).astype(f32)
    return high, middle, rest - middle


def column_step(mult_ref, ids_ref, cost_ref, inc_pair, prev, rows_scr, parts_scr, mean_ref, soft_ref, cover_ref):
    tiles = cost_ref.shape[0]
    for t in range(tiles):
        for k in range(K):
            at = (t // 8 * K + k) * 8 + t % 8
            rows_scr[at : at + 1, :] = mult_ref[pl.ds(ids_ref[k, t], 1), :]
    parts_scr[...] = jnp.zeros_like(parts_scr)
    cover_ref[...] = jnp.zeros_like(cover_ref)
    line = lax.broadcasted_iota(jnp.int32, (8, BLK), 0)
    none = jnp.zeros((8, BLK), f32)
    soft_sum = none
    for group in range(tiles // 8):
        parts = [
            three_parts(rows_scr[(group * K + k) * 8 : (group * K + k + 1) * 8, :]) for k in range(K)
        ]
        acc = jnp.zeros((32, 2 * TILE), f32)
        for q in range(4):
            keep = line % 4 == q
            lhs = [
                jnp.concatenate([jnp.where(keep, p, 0.0) for p in parts[k]] + [none], axis=0)
                for k in range(K)
            ]
            lhs = jnp.concatenate(lhs, axis=1).astype(bf16)
            acc += jnp.dot(lhs, inc_pair(group, q), preferred_element_type=f32)
        here = slice(group * 8, group * 8 + 8)
        both = acc[:8] + acc[8:16] + acc[16:24]
        priced = jnp.where(line < 4, both[:, :TILE], both[:, TILE:])
        reduced = cost_ref[here, :].astype(f32) - priced
        scaled = reduced / 8.0
        primal = 1.0 / (1.0 + jnp.exp(scaled))
        soft_sum += -8.0 * (jnp.maximum(-scaled, 0.0) + jnp.log1p(jnp.exp(-jnp.abs(scaled))))
        mean = primal if prev is None else 0.3 * primal + 0.7 * prev[here, :]
        mean_ref[here, :] = mean
        for s, p in enumerate(three_parts(mean)):
            parts_scr[pl.ds(group * 64 + s, 4, stride=8), :] = p[:4]
            parts_scr[pl.ds(group * 64 + 35 + s, 4, stride=8), :] = p[4:]
        for q in range(4):
            at = group * 64 + q * 8
            lhs = [parts_scr[at : at + 8, :], parts_scr[at + 32 : at + 40, :]]
            out = lax.dot_general(
                jnp.concatenate(lhs, axis=1).astype(bf16),
                inc_pair(group, q),
                (((1,), (1,)), ((), ())),
                preferred_element_type=f32,
            )
            for row, t in ((0, group * 8 + q), (3, group * 8 + q + 4)):
                part = out[row : row + 1] + out[row + 1 : row + 2] + out[row + 2 : row + 3]
                for k in range(K):
                    cover_ref[pl.ds(ids_ref[k, t], 1), :] += part[:, k * BLK : (k + 1) * BLK]
    soft_ref[...] = soft_sum


def first_kernel(
    ids_hbm, inc_hbm, cost_hbm, mult_hbm, inc_ref, mean_ref, soft_ref, cover_ref, sum_ref,
    ids, raw, cost, mult, rows_scr, parts_scr, sems,
):
    tiles = cost.shape[0]
    small = [
        pltpu.make_async_copy(src, dst, sems.at[tiles + i])
        for i, (src, dst) in enumerate(((ids_hbm, ids), (mult_hbm, mult), (cost_hbm, cost)))
    ]
    large = [pltpu.make_async_copy(inc_hbm.at[t], raw.at[t], sems.at[t]) for t in range(tiles)]
    for copy in small:
        copy.start()
    for group in range(0, tiles, 8):
        for q in range(4):
            large[group + q].start()
            large[group + q + 4].start()
    for copy in small:
        copy.wait()
    seen = set()

    def inc_pair(group, q):
        pair = group * 4 + q
        if pair not in seen:
            seen.add(pair)
            for side in range(2):
                t = group * 8 + side * 4 + q
                large[t].wait()
                inc_ref[pair, :, side * TILE : (side + 1) * TILE] = (
                    raw[t].reshape(K * BLK, TILE).astype(f32).astype(inc_ref.dtype)
                )
        return inc_ref[pair]

    column_step(mult, ids, cost, inc_pair, None, rows_scr, parts_scr, mean_ref, soft_ref, cover_ref)
    sum_ref[...] = total_of(mult[...])


def total_of(v):
    n = v.shape[0] // 8
    v = v.reshape(n, 8, BLK)
    chains = [v[i] for i in range(4)]
    for i in range(4, n):
        chains[i % 4] = chains[i % 4] + v[i]
    return (chains[0] + chains[1]) + (chains[2] + chains[3])


def row_step(own_ref, other_ref, mult_ref, sum_ref, upper_ref, new_ref):
    me = lax.axis_index("c")
    half = mult_ref.shape[0] // 2
    slopes, soft, norm = [], sum_ref[...], 0.0
    for ref in (own_ref, other_ref):
        slope = 1.0 - ref[:, : SLOT - 8, :].reshape(half, BLK)
        slopes.append(slope)
        norm = norm + total_of(slope * slope)
        soft = soft + total_of(ref[:, SLOT - 8 :, :].reshape(half // 2, BLK))
    value = jnp.sum(soft, keepdims=True)
    size = (upper_ref[0] - value) / (jnp.sum(norm, keepdims=True) + 1e-06)
    for slope, core in zip(slopes, (me, 1 - me)):
        at = pl.ds(pl.multiple_of(core * half, half), half)
        new_ref[at, :] = jnp.maximum(0.0, mult_ref[at, :] + size * slope)


def next_kernel(
    own_ref, other_ref, mult_ref, sum_ref, upper_ref, ids_ref, inc_ref, cost_ref, prev_ref,
    new_ref, mean_ref, soft_ref, cover_ref, total_ref, rows_scr, parts_scr,
):
    row_step(own_ref, other_ref, mult_ref, sum_ref, upper_ref, new_ref)
    column_step(
        new_ref, ids_ref, cost_ref, lambda group, q: inc_ref[group * 4 + q],
        prev_ref, rows_scr, parts_scr, mean_ref, soft_ref, cover_ref,
    )
    total_ref[...] = total_of(new_ref[...])


def last_kernel(own_ref, other_ref, mult_ref, sum_ref, upper_ref, mean_ref, new_ref, out_ref):
    out_ref[...] = mean_ref[...]
    row_step(own_ref, other_ref, mult_ref, sum_ref, upper_ref, new_ref)


def owner_kernel(in_ref, soft_ref, out_ref):
    total = in_ref[0]
    for i in range(1, in_ref.shape[0]):
        total += in_ref[i]
    for i in range(out_ref.shape[0]):
        out_ref[i, : SLOT - 8] = total
        out_ref[i, SLOT - 8 :] = soft_ref[...]


def spread_kernel(in_ref, out_ref):
    total = in_ref[0]
    for i in range(1, in_ref.shape[0]):
        total += in_ref[i]
    for i in range(out_ref.shape[0]):
        out_ref[i] = total


def call(kernel, name, out, specs, scratch=(), mib=8):
    return pl.pallas_call(
        kernel,
        out_shape=out,
        in_specs=specs,
        out_specs=jax.tree.map(lambda _: VMEM, out),
        scratch_shapes=scratch,
        compiler_params=pltpu.CompilerParams(vmem_limit_bytes=mib << 20),
        name=name,
    )


def local(block_ids, incidence, costs, start_mult, upper):
    tiles, rows = block_ids.shape[0], start_mult.shape[0]
    sds = jax.ShapeDtypeStruct
    ids = block_ids.T
    tile_sums, multipliers, columns = sds((8, TILE), f32), sds((rows, BLK), f32), sds((tiles, TILE), f32)
    outs = (columns, tile_sums, multipliers, tile_sums)
    scratch = [pltpu.VMEM((tiles * K, BLK), f32), pltpu.VMEM((tiles * 8, TILE), f32)]
    inc, mean, soft, cover, total = call(
        first_kernel,
        "first",
        (sds((tiles // 2, K * BLK, 2 * TILE), INC), *outs),
        [HBM] * 4,
        [
            pltpu.SMEM((K, tiles), jnp.int32),
            pltpu.VMEM((tiles, K, BLK, TILE), jnp.int32),
            pltpu.VMEM((tiles, TILE), jnp.int32),
            pltpu.VMEM((rows, BLK), f32),
            *scratch,
            pltpu.SemaphoreType.DMA((tiles + 3,)),
        ],
        mib=16,
    )(*(pltpu.with_memory_space_constraint(a, pltpu.HBM) for a in (ids, incidence, costs, start_mult)))
    mult = start_mult
    for step in range(ITERS):
        there = lax.all_to_all(cover.reshape(C * X * Y, SLOT - 8, BLK), OWNERS, 0, 0, tiled=True)
        there = call(owner_kernel, "owner", sds((Z, SLOT, BLK), f32), [VMEM] * 2)(there, soft)
        there = lax.all_to_all(there, "z", 0, 0, tiled=True)
        there = call(spread_kernel, "spread", sds((X * Y, SLOT, BLK), f32), [VMEM])(there)
        own = lax.all_to_all(there, NEAR, 0, 0, tiled=True)
        other = lax.ppermute(own, "c", [(0, 1), (1, 0)])
        rows_in = (own, other, mult, total, upper)
        if step < ITERS - 1:
            mult, mean, soft, cover, total = call(
                next_kernel,
                "next",
                (multipliers, *outs),
                [VMEM] * 4 + [SMEM] * 2 + [VMEM] * 3,
                scratch,
            )(*rows_in, ids, inc, costs, mean)
    return call(last_kernel, "last", (multipliers, columns), [VMEM] * 4 + [SMEM, VMEM])(*rows_in, mean)


def solution(mesh):
    split = Mesh(mesh.devices.reshape(X, C, Y, Z), SPLIT)
    return jax.shard_map(
        local,
        mesh=split,
        in_specs=(
            P(SPLIT, None),
            P(SPLIT, None, None, None),
            P(SPLIT, None),
            P(),
            P(),
        ),
        out_specs=(P(), P(SPLIT, None)),
        check_vma=False,
    )
```

time: 131 us -> 131 us (level)
  no operation moved by 1% of the time
where the time goes in v3:
time: 131 us
  blocking collectives  108 us (82%)
  Pallas kernels  9.4 us (7%)
  starting transfers between devices  9.39 us (7%)
  waiting for transfers between devices  2.56 us (2%)
  between operations  1.36 us (1%)
    all_to_all x3, blocking collectives, local(): lax.all_to_all(cover.reshape(C * X * Y, SLOT - 8, BLK), OWNERS, 0, 0, til...  42.7 us
    all_to_all x3, blocking collectives, local(): there = lax.all_to_all(there, 'z', 0, 0, tiled=True)  35.2 us
    all_to_all x3, blocking collectives, local(): own = lax.all_to_all(there, NEAR, 0, 0, tiled=True)  30.1 us
    ppermute x3, starting transfers between devices, local(): other = lax.ppermute(own, 'c', [(0, 1), (1, 0)])  9.39 us
    pallas_call x2, Pallas kernels, local(): call(next_kernel, 'next', (multipliers, *outs), [VMEM] * 4 + [SMEM] * 2 +...  4.33 us
    pallas_call x1, Pallas kernels, local(): call(first_kernel, 'first', (sds((tiles // 2, K * BLK, 2 * TILE), INC), *...  3.99 us
  transfers between devices with their start and end apart: 3, of which 3 were waited for; matrix products, arithmetic and copies ran while one was open for 0% of the time, Pallas kernels for 0%

profile of v3, /device:TPU:1, one launch (start us, length us, event | category | flops | bytes accessed | tf_op | source)
XLA Modules:
  0.0 130.7 jit_solution(11114898183259138161)
XLA Ops:
  0.6 0.0 copy-start.1
  0.6 0.0 copy-start
  0.7 0.0 copy-start.2
  0.7 4.0 %first.1 = (bf16[8,512,256]{2,1,0:T(8,128)(2,1)S(1)}, f32[16,128]{1,0:T(8,128)S(1)}, f32[8,128]{1,0:T(8,128)S(1)}, f32[512,128]{1,0:T(8,128)S(1)}, f32[8,128]{1,0:T(8,128)S(1)}) custom-call(s32[4,16]{1,0:T(4,128)} %bitcast.7, s32[16,4,128,128]{3,2,1,0:T(8,128)} %inc_hbm.1, s32[16,128]{1,0:T(8,128)} %cost_ref.3, f32[512,128]{1,0:T(8,128)} %mult_ref.1), custom_call_target="tpu_custom_call" | custom-call | tf_op jit(solution)/shard_map/first/pallas_call | solution.py:199
  4.7 17.2 %all_to_all.45.in_ref = f32[32,16,128]{2,1,0:T(8,128)S(1)} all-to-all(f32[32,16,128]{2,1,0:T(8,128)S(1)} %bitcast.6), channel_id=1, replica_groups=mesh['x'=4,'c'=2,'y'=4,'z'=8] {'c','x','y'}, dimensions={0} | all-to-all | bytes 524288 | tf_op jit(solution)/shard_map/all_to_all | solution.py:216
  21.9 15.6 %all_to_all.46.in_ref = f32[8,24,128]{2,1,0:T(8,128)S(1)} all-to-all(f32[8,24,128]{2,1,0:T(8,128)S(1)} %owner.3), channel_id=1, replica_groups=mesh['x'=4,'c'=2,'y'=4,'z'=8] {'z'}, dimensions={0} | all-to-all | bytes 196608 | tf_op jit(solution)/shard_map/all_to_all | solution.py:218
  37.5 9.9 %all_to_all.47.own_ref = f32[16,24,128]{2,1,0:T(8,128)S(1)} all-to-all(f32[16,24,128]{2,1,0:T(8,128)S(1)} %spread.3), channel_id=1, replica_groups=mesh['x'=4,'c'=2,'y'=4,'z'=8] {'x','y'}, dimensions={0} | all-to-all | bytes 393216 | tf_op jit(solution)/shard_map/all_to_all | solution.py:220
  47.4 3.2 %collective-permute-start = (f32[16,24,128]{2,1,0:T(8,128)S(1)}, f32[16,24,128]{2,1,0:T(8,128)S(1)}, u32[]{:S(2)}, u32[]{:S(2)}) collective-permute-start(f32[16,24,128]{2,1,0:T(8,128)S(1)} %all_to_all.47.own_ref), channel_id=1, source_target_pairs={{0,32},{32,0},{1,33},{33,1},{2,34},{34,2},{3,35},{35,3},{4,36},{36... | collective-permute-start | bytes 589832 | tf_op jit(solution)/shard_map/ppermute | solution.py:221
  51.3 0.4 collective-permute-done.other_ref
  51.7 0.0 copy-done.1
  51.7 0.0 copy-done
  51.7 0.0 copy-done.2
  51.7 2.2 %next.2 = (f32[512,128]{1,0:T(8,128)S(1)}, f32[16,128]{1,0:T(8,128)S(1)}, f32[8,128]{1,0:T(8,128)S(1)}, f32[512,128]{1,0:T(8,128)S(1)}, f32[8,128]{1,0:T(8,128)S(1)}) custom-call(f32[16,24,128]{2,1,0:T(8,128)S(1)} %all_to_all.47.own_ref, f32[16,24,128]{2,1,0:T(8,128)S(1)} %collective-permute-done.other_ref, f32[512,128]{1,0:T(8,128)S(1)} %copy-done, ...), custom_call_target="tpu_custom_call" | custom-call | tf_op jit(solution)/shard_map/next/pallas_call | solution.py:224
  53.9 12.8 %all_to_all.48.in_ref = f32[32,16,128]{2,1,0:T(8,128)S(1)} all-to-all(f32[32,16,128]{2,1,0:T(8,128)S(1)} %bitcast.5), channel_id=1, replica_groups=mesh['x'=4,'c'=2,'y'=4,'z'=8] {'c','x','y'}, dimensions={0} | all-to-all | bytes 524288 | tf_op jit(solution)/shard_map/all_to_all | solution.py:216
  66.7 9.8 %all_to_all.49.in_ref = f32[8,24,128]{2,1,0:T(8,128)S(1)} all-to-all(f32[8,24,128]{2,1,0:T(8,128)S(1)} %owner.4), channel_id=1, replica_groups=mesh['x'=4,'c'=2,'y'=4,'z'=8] {'z'}, dimensions={0} | all-to-all | bytes 196608 | tf_op jit(solution)/shard_map/all_to_all | solution.py:218
  76.6 10.1 %all_to_all.50.own_ref = f32[16,24,128]{2,1,0:T(8,128)S(1)} all-to-all(f32[16,24,128]{2,1,0:T(8,128)S(1)} %spread.4), channel_id=1, replica_groups=mesh['x'=4,'c'=2,'y'=4,'z'=8] {'x','y'}, dimensions={0} | all-to-all | bytes 393216 | tf_op jit(solution)/shard_map/all_to_all | solution.py:220
  86.6 3.1 %collective-permute-start.1 = (f32[16,24,128]{2,1,0:T(8,128)S(1)}, f32[16,24,128]{2,1,0:T(8,128)S(1)}, u32[]{:S(2)}, u32[]{:S(2)}) collective-permute-start(f32[16,24,128]{2,1,0:T(8,128)S(1)} %all_to_all.50.own_ref), channel_id=1, source_target_pairs={{0,32},{32,0},{1,33},{33,1},{2,34},{34,2},{3,35},{35,3},{4,36},{36... | collective-permute-start | bytes 589832 | tf_op jit(solution)/shard_map/ppermute | solution.py:221
  89.7 1.1 collective-permute-done.1.other_ref
  90.8 2.2 %next.3 = (f32[512,128]{1,0:T(8,128)S(1)}, f32[16,128]{1,0:T(8,128)S(1)}, f32[8,128]{1,0:T(8,128)S(1)}, f32[512,128]{1,0:T(8,128)S(1)}, f32[8,128]{1,0:T(8,128)S(1)}) custom-call(f32[16,24,128]{2,1,0:T(8,128)S(1)} %all_to_all.50.own_ref, f32[16,24,128]{2,1,0:T(8,128)S(1)} %collective-permute-done.1.other_ref, f32[512,128]{1,0:T(8,128)S(1)} %get-tuple-element.24.mult_ref, ...), custom_call_target="tpu_custom_call" | custom-call | tf_op jit(solution)/shard_map/next/pallas_call | solution.py:224
  93.0 12.8 %all_to_all.51.in_ref = f32[32,16,128]{2,1,0:T(8,128)S(1)} all-to-all(f32[32,16,128]{2,1,0:T(8,128)S(1)} %bitcast.4), channel_id=1, replica_groups=mesh['x'=4,'c'=2,'y'=4,'z'=8] {'c','x','y'}, dimensions={0} | all-to-all | bytes 524288 | tf_op jit(solution)/shard_map/all_to_all | solution.py:216
  105.8 9.8 %all_to_all.52.in_ref = f32[8,24,128]{2,1,0:T(8,128)S(1)} all-to-all(f32[8,24,128]{2,1,0:T(8,128)S(1)} %owner.5), channel_id=1, replica_groups=mesh['x'=4,'c'=2,'y'=4,'z'=8] {'z'}, dimensions={0} | all-to-all | bytes 196608 | tf_op jit(solution)/shard_map/all_to_all | solution.py:218
  115.6 10.1 %all_to_all.53.own_ref = f32[16,24,128]{2,1,0:T(8,128)S(1)} all-to-all(f32[16,24,128]{2,1,0:T(8,128)S(1)} %spread.5), channel_id=1, replica_groups=mesh['x'=4,'c'=2,'y'=4,'z'=8] {'x','y'}, dimensions={0} | all-to-all | bytes 393216 | tf_op jit(solution)/shard_map/all_to_all | solution.py:220
  125.7 3.1 %collective-permute-start.2 = (f32[16,24,128]{2,1,0:T(8,128)S(1)}, f32[16,24,128]{2,1,0:T(8,128)S(1)}, u32[]{:S(2)}, u32[]{:S(2)}) collective-permute-start(f32[16,24,128]{2,1,0:T(8,128)S(1)} %all_to_all.53.own_ref), channel_id=1, source_target_pairs={{0,32},{32,0},{1,33},{33,1},{2,34},{34,2},{3,35},{35,3},{4,36},{36... | collective-permute-start | bytes 589832 | tf_op jit(solution)/shard_map/ppermute | solution.py:221
  128.8 1.1 collective-permute-done.2.other_ref
  129.8 0.9 last.1
  (6 shorter events, 0.2 us)
Async XLA Ops:
  0.6 51.1 %copy-start.1 = (s32[16,128]{1,0:T(8,128)S(1)}, s32[16,128]{1,0:T(8,128)}, u32[]{:S(2)}) copy-start(s32[16,128]{1,0:T(8,128)} %cost_ref.3) | copy-start | bytes 24580
  0.6 51.1 %copy-start = (f32[512,128]{1,0:T(8,128)S(1)}, f32[512,128]{1,0:T(8,128)}, u32[]{:S(2)}) copy-start(f32[512,128]{1,0:T(8,128)} %mult_ref.1) | copy-start | bytes 786436
  0.7 51.1 %copy-start.2 = (s32[16,4]{0,1:T(4,128)S(1)}, s32[16,4]{0,1:T(4,128)}, u32[]{:S(2)}) copy-start(s32[16,4]{0,1:T(4,128)} %param.5) | copy-start | bytes 772
  47.4 4.3 %collective-permute-start = (f32[16,24,128]{2,1,0:T(8,128)S(1)}, f32[16,24,128]{2,1,0:T(8,128)S(1)}, u32[]{:S(2)}, u32[]{:S(2)}) collective-permute-start(f32[16,24,128]{2,1,0:T(8,128)S(1)} %all_to_all.47.own_ref), channel_id=1, source_target_pairs={{0,32},{32,0},{1,33},{33,1},{2,34},{34,2},{3,35},{35,3},{4,36},{36... | collective-permute-start | bytes 589832 | tf_op jit(solution)/shard_map/ppermute | solution.py:221
  86.6 4.2 %collective-permute-start.1 = (f32[16,24,128]{2,1,0:T(8,128)S(1)}, f32[16,24,128]{2,1,0:T(8,128)S(1)}, u32[]{:S(2)}, u32[]{:S(2)}) collective-permute-start(f32[16,24,128]{2,1,0:T(8,128)S(1)} %all_to_all.50.own_ref), channel_id=1, source_target_pairs={{0,32},{32,0},{1,33},{33,1},{2,34},{34,2},{3,35},{35,3},{4,36},{36... | collective-permute-start | bytes 589832 | tf_op jit(solution)/shard_map/ppermute | solution.py:221
  125.7 4.2 %collective-permute-start.2 = (f32[16,24,128]{2,1,0:T(8,128)S(1)}, f32[16,24,128]{2,1,0:T(8,128)S(1)}, u32[]{:S(2)}, u32[]{:S(2)}) collective-permute-start(f32[16,24,128]{2,1,0:T(8,128)S(1)} %all_to_all.53.own_ref), channel_id=1, source_target_pairs={{0,32},{32,0},{1,33},{33,1},{2,34},{34,2},{3,35},{35,3},{4,36},{36... | collective-permute-start | bytes 589832 | tf_op jit(solution)/shard_map/ppermute | solution.py:221

commit v4 on v3

--- a/solution.py
+++ b/solution.py
@@ -17,7 +17,7 @@
 SLOT = 24
 
 f32, bf16 = jnp.float32, jnp.bfloat16
-INC = bf16
+INC = jnp.float8_e4m3fn
 VMEM = pl.BlockSpec(memory_space=pltpu.VMEM)
 SMEM = pl.BlockSpec(memory_space=pltpu.SMEM)
 HBM = pl.BlockSpec(memory_space=pltpu.HBM)

time: 131 us -> 130 us (level)
  Pallas kernels: 9.4 us -> 7.87 us
where the time goes in v4:
time: 130 us; the launch traced here: 129 us
  blocking collectives  108 us (83%)
  starting transfers between devices  9.39 us (7%)
  Pallas kernels  7.87 us (6%)
  waiting for transfers between devices  2.56 us (2%)
  between operations  1.36 us (1%)
    all_to_all x3, blocking collectives, local(): lax.all_to_all(cover.reshape(C * X * Y, SLOT - 8, BLK), OWNERS, 0, 0, til...  42.7 us
    all_to_all x3, blocking collectives, local(): there = lax.all_to_all(there, 'z', 0, 0, tiled=True)  35.2 us
    all_to_all x3, blocking collectives, local(): own = lax.all_to_all(there, NEAR, 0, 0, tiled=True)  30.1 us
    ppermute x3, starting transfers between devices, local(): other = lax.ppermute(own, 'c', [(0, 1), (1, 0)])  9.39 us
    pallas_call x2, Pallas kernels, local(): call(next_kernel, 'next', (multipliers, *outs), [VMEM] * 4 + [SMEM] * 2 +...  3.45 us
    pallas_call x1, Pallas kernels, local(): call(first_kernel, 'first', (sds((tiles // 2, K * BLK, 2 * TILE), INC), *...  3.33 us
  transfers between devices with their start and end apart: 3, of which 3 were waited for; matrix products, arithmetic and copies ran while one was open for 0% of the time, Pallas kernels for 0%

profile of v4, /device:TPU:1, one launch (start us, length us, event | category | flops | bytes accessed | tf_op | source)
XLA Modules:
  0.0 129.2 jit_solution(5208804637243121187)
XLA Ops:
  0.6 0.0 copy-start.1
  0.6 0.0 copy-start
  0.7 0.0 copy-start.2
  0.7 3.3 %first.1 = (f8e4m3fn[8,512,256]{2,1,0:T(32,128)(4,1)S(1)}, f32[16,128]{1,0:T(8,128)S(1)}, f32[8,128]{1,0:T(8,128)S(1)}, f32[512,128]{1,0:T(8,128)S(1)}, f32[8,128]{1,0:T(8,128)S(1)}) custom-call(s32[4,16]{1,0:T(4,128)} %bitcast.7, s32[16,4,128,128]{3,2,1,0:T(8,128)} %inc_hbm.1, s32[16,128]{1,0:T(8,128)} %cost_ref.3, f32[512,128]{1,0:T(8,128)} %mult_ref.1), custom_call_target="tpu_custom_call" | custom-call | tf_op jit(solution)/shard_map/first/pallas_call | solution.py:199
  4.0 17.2 %all_to_all.45.in_ref = f32[32,16,128]{2,1,0:T(8,128)S(1)} all-to-all(f32[32,16,128]{2,1,0:T(8,128)S(1)} %bitcast.6), channel_id=1, replica_groups=mesh['x'=4,'c'=2,'y'=4,'z'=8] {'c','x','y'}, dimensions={0} | all-to-all | bytes 524288 | tf_op jit(solution)/shard_map/all_to_all | solution.py:216
  21.2 15.6 %all_to_all.46.in_ref = f32[8,24,128]{2,1,0:T(8,128)S(1)} all-to-all(f32[8,24,128]{2,1,0:T(8,128)S(1)} %owner.3), channel_id=1, replica_groups=mesh['x'=4,'c'=2,'y'=4,'z'=8] {'z'}, dimensions={0} | all-to-all | bytes 196608 | tf_op jit(solution)/shard_map/all_to_all | solution.py:218
  36.9 9.9 %all_to_all.47.own_ref = f32[16,24,128]{2,1,0:T(8,128)S(1)} all-to-all(f32[16,24,128]{2,1,0:T(8,128)S(1)} %spread.3), channel_id=1, replica_groups=mesh['x'=4,'c'=2,'y'=4,'z'=8] {'x','y'}, dimensions={0} | all-to-all | bytes 393216 | tf_op jit(solution)/shard_map/all_to_all | solution.py:220
  46.8 3.2 %collective-permute-start = (f32[16,24,128]{2,1,0:T(8,128)S(1)}, f32[16,24,128]{2,1,0:T(8,128)S(1)}, u32[]{:S(2)}, u32[]{:S(2)}) collective-permute-start(f32[16,24,128]{2,1,0:T(8,128)S(1)} %all_to_all.47.own_ref), channel_id=1, source_target_pairs={{0,32},{32,0},{1,33},{33,1},{2,34},{34,2},{3,35},{35,3},{4,36},{36... | collective-permute-start | bytes 589832 | tf_op jit(solution)/shard_map/ppermute | solution.py:221
  50.6 0.4 collective-permute-done.other_ref
  51.1 0.0 copy-done.1
  51.1 0.0 copy-done
  51.1 0.0 copy-done.2
  51.1 1.7 %next.2 = (f32[512,128]{1,0:T(8,128)S(1)}, f32[16,128]{1,0:T(8,128)S(1)}, f32[8,128]{1,0:T(8,128)S(1)}, f32[512,128]{1,0:T(8,128)S(1)}, f32[8,128]{1,0:T(8,128)S(1)}) custom-call(f32[16,24,128]{2,1,0:T(8,128)S(1)} %all_to_all.47.own_ref, f32[16,24,128]{2,1,0:T(8,128)S(1)} %collective-permute-done.other_ref, f32[512,128]{1,0:T(8,128)S(1)} %copy-done, ...), custom_call_target="tpu_custom_call" | custom-call | tf_op jit(solution)/shard_map/next/pallas_call | solution.py:224
  52.8 12.8 %all_to_all.48.in_ref = f32[32,16,128]{2,1,0:T(8,128)S(1)} all-to-all(f32[32,16,128]{2,1,0:T(8,128)S(1)} %bitcast.5), channel_id=1, replica_groups=mesh['x'=4,'c'=2,'y'=4,'z'=8] {'c','x','y'}, dimensions={0} | all-to-all | bytes 524288 | tf_op jit(solution)/shard_map/all_to_all | solution.py:216
  65.6 9.8 %all_to_all.49.in_ref = f32[8,24,128]{2,1,0:T(8,128)S(1)} all-to-all(f32[8,24,128]{2,1,0:T(8,128)S(1)} %owner.4), channel_id=1, replica_groups=mesh['x'=4,'c'=2,'y'=4,'z'=8] {'z'}, dimensions={0} | all-to-all | bytes 196608 | tf_op jit(solution)/shard_map/all_to_all | solution.py:218
  75.5 10.1 %all_to_all.50.own_ref = f32[16,24,128]{2,1,0:T(8,128)S(1)} all-to-all(f32[16,24,128]{2,1,0:T(8,128)S(1)} %spread.4), channel_id=1, replica_groups=mesh['x'=4,'c'=2,'y'=4,'z'=8] {'x','y'}, dimensions={0} | all-to-all | bytes 393216 | tf_op jit(solution)/shard_map/all_to_all | solution.py:220
  85.5 3.1 %collective-permute-start.1 = (f32[16,24,128]{2,1,0:T(8,128)S(1)}, f32[16,24,128]{2,1,0:T(8,128)S(1)}, u32[]{:S(2)}, u32[]{:S(2)}) collective-permute-start(f32[16,24,128]{2,1,0:T(8,128)S(1)} %all_to_all.50.own_ref), channel_id=1, source_target_pairs={{0,32},{32,0},{1,33},{33,1},{2,34},{34,2},{3,35},{35,3},{4,36},{36... | collective-permute-start | bytes 589832 | tf_op jit(solution)/shard_map/ppermute | solution.py:221
  88.6 1.1 collective-permute-done.1.other_ref
  89.7 1.7 %next.3 = (f32[512,128]{1,0:T(8,128)S(1)}, f32[16,128]{1,0:T(8,128)S(1)}, f32[8,128]{1,0:T(8,128)S(1)}, f32[512,128]{1,0:T(8,128)S(1)}, f32[8,128]{1,0:T(8,128)S(1)}) custom-call(f32[16,24,128]{2,1,0:T(8,128)S(1)} %all_to_all.50.own_ref, f32[16,24,128]{2,1,0:T(8,128)S(1)} %collective-permute-done.1.other_ref, f32[512,128]{1,0:T(8,128)S(1)} %get-tuple-element.24.mult_ref, ...), custom_call_target="tpu_custom_call" | custom-call | tf_op jit(solution)/shard_map/next/pallas_call | solution.py:224
  91.4 12.8 %all_to_all.51.in_ref = f32[32,16,128]{2,1,0:T(8,128)S(1)} all-to-all(f32[32,16,128]{2,1,0:T(8,128)S(1)} %bitcast.4), channel_id=1, replica_groups=mesh['x'=4,'c'=2,'y'=4,'z'=8] {'c','x','y'}, dimensions={0} | all-to-all | bytes 524288 | tf_op jit(solution)/shard_map/all_to_all | solution.py:216
  104.2 9.8 %all_to_all.52.in_ref = f32[8,24,128]{2,1,0:T(8,128)S(1)} all-to-all(f32[8,24,128]{2,1,0:T(8,128)S(1)} %owner.5), channel_id=1, replica_groups=mesh['x'=4,'c'=2,'y'=4,'z'=8] {'z'}, dimensions={0} | all-to-all | bytes 196608 | tf_op jit(solution)/shard_map/all_to_all | solution.py:218
  114.1 10.1 %all_to_all.53.own_ref = f32[16,24,128]{2,1,0:T(8,128)S(1)} all-to-all(f32[16,24,128]{2,1,0:T(8,128)S(1)} %spread.5), channel_id=1, replica_groups=mesh['x'=4,'c'=2,'y'=4,'z'=8] {'x','y'}, dimensions={0} | all-to-all | bytes 393216 | tf_op jit(solution)/shard_map/all_to_all | solution.py:220
  124.1 3.1 %collective-permute-start.2 = (f32[16,24,128]{2,1,0:T(8,128)S(1)}, f32[16,24,128]{2,1,0:T(8,128)S(1)}, u32[]{:S(2)}, u32[]{:S(2)}) collective-permute-start(f32[16,24,128]{2,1,0:T(8,128)S(1)} %all_to_all.53.own_ref), channel_id=1, source_target_pairs={{0,32},{32,0},{1,33},{33,1},{2,34},{34,2},{3,35},{35,3},{4,36},{36... | collective-permute-start | bytes 589832 | tf_op jit(solution)/shard_map/ppermute | solution.py:221
  127.2 1.1 collective-permute-done.2.other_ref
  128.3 0.9 last.1
  (6 shorter events, 0.2 us)
Async XLA Ops:
  0.6 50.4 %copy-start.1 = (s32[16,128]{1,0:T(8,128)S(1)}, s32[16,128]{1,0:T(8,128)}, u32[]{:S(2)}) copy-start(s32[16,128]{1,0:T(8,128)} %cost_ref.3) | copy-start | bytes 24580
  0.6 50.4 %copy-start = (f32[512,128]{1,0:T(8,128)S(1)}, f32[512,128]{1,0:T(8,128)}, u32[]{:S(2)}) copy-start(f32[512,128]{1,0:T(8,128)} %mult_ref.1) | copy-start | bytes 786436
  0.7 50.4 %copy-start.2 = (s32[16,4]{0,1:T(4,128)S(1)}, s32[16,4]{0,1:T(4,128)}, u32[]{:S(2)}) copy-start(s32[16,4]{0,1:T(4,128)} %param.5) | copy-start | bytes 772
  46.8 4.3 %collective-permute-start = (f32[16,24,128]{2,1,0:T(8,128)S(1)}, f32[16,24,128]{2,1,0:T(8,128)S(1)}, u32[]{:S(2)}, u32[]{:S(2)}) collective-permute-start(f32[16,24,128]{2,1,0:T(8,128)S(1)} %all_to_all.47.own_ref), channel_id=1, source_target_pairs={{0,32},{32,0},{1,33},{33,1},{2,34},{34,2},{3,35},{35,3},{4,36},{36... | collective-permute-start | bytes 589832 | tf_op jit(solution)/shard_map/ppermute | solution.py:221
  85.5 4.2 %collective-permute-start.1 = (f32[16,24,128]{2,1,0:T(8,128)S(1)}, f32[16,24,128]{2,1,0:T(8,128)S(1)}, u32[]{:S(2)}, u32[]{:S(2)}) collective-permute-start(f32[16,24,128]{2,1,0:T(8,128)S(1)} %all_to_all.50.own_ref), channel_id=1, source_target_pairs={{0,32},{32,0},{1,33},{33,1},{2,34},{34,2},{3,35},{35,3},{4,36},{36... | collective-permute-start | bytes 589832 | tf_op jit(solution)/shard_map/ppermute | solution.py:221
  124.1 4.2 %collective-permute-start.2 = (f32[16,24,128]{2,1,0:T(8,128)S(1)}, f32[16,24,128]{2,1,0:T(8,128)S(1)}, u32[]{:S(2)}, u32[]{:S(2)}) collective-permute-start(f32[16,24,128]{2,1,0:T(8,128)S(1)} %all_to_all.53.own_ref), channel_id=1, source_target_pairs={{0,32},{32,0},{1,33},{33,1},{2,34},{34,2},{3,35},{35,3},{4,36},{36... | collective-permute-start | bytes 589832 | tf_op jit(solution)/shard_map/ppermute | solution.py:221

commit v5 on v4

v5 whole, which is shorter than its diff:
```python
import jax
import jax.numpy as jnp
from jax import lax
from jax.experimental import pallas as pl
from jax.experimental.pallas import tpu as pltpu
from jax.sharding import Mesh
from jax.sharding import PartitionSpec as P

BLK = 128
TILE = 128
K = 4
ITERS = 3
X, C, Y, Z = 4, 2, 4, 8
NEAR, FAR = X * Y, Z
OWN = 16
SLOT = OWN + 8
PLANE_ORDER = (
    (1, 2), (2, 2), (0, 2), (0, 1), (3, 3), (2, 3), (0, 3), (0, 0),
    (3, 2), (1, 0), (1, 3), (3, 1), (2, 1), (1, 1), (2, 0), (3, 0),
)
LINE_ORDER = (0, 2, 4, 6, 7, 1, 3, 5)


def device(x, c, y, z):
    return ((x * C + c) * Y + y) * Z + z


PLANES = [[device(x, c, y, z) for x, y in PLANE_ORDER] for c in range(C) for z in range(Z)]
LINES = [
    [device(x, c, y, z) for z in LINE_ORDER] for x in range(X) for c in range(C) for y in range(Y)
]
SWAP = [
    (device(x, c, y, z), device(x, 1 - c, y, z))
    for x in range(X)
    for c in range(C)
    for y in range(Y)
    for z in range(Z)
]

f32, bf16 = jnp.float32, jnp.bfloat16
INC = jnp.float8_e4m3fn
VMEM = pl.BlockSpec(memory_space=pltpu.VMEM)
SMEM = pl.BlockSpec(memory_space=pltpu.SMEM)
ANY = pl.BlockSpec(memory_space=pl.ANY)
HBM = pl.BlockSpec(memory_space=pltpu.HBM)


def my_core():
    return (lax.axis_index("d") >> 5) & 1


def three_parts(v):
    high = v.astype(bf16).astype(f32)
    rest = v - high
    middle = rest.astype(bf16).astype(f32)
    return high, middle, rest - middle


def column_step(mult_ref, ids_ref, cost_ref, inc_pair, prev, rows_scr, parts_scr, cover_scr, mean_ref, soft_ref, mine_ref, send_ref):
    tiles = cost_ref.shape[0]
    for t in range(tiles):
        for k in range(K):
            at = (t // 8 * K + k) * 8 + t % 8
            rows_scr[at : at + 1, :] = mult_ref[pl.ds(ids_ref[k, t], 1), :]
    parts_scr[...] = jnp.zeros_like(parts_scr)
    cover_scr[...] = jnp.zeros_like(cover_scr)
    half = mine_ref.shape[0]
    turn = my_core() * half
    line = lax.broadcasted_iota(jnp.int32, (8, BLK), 0)
    none = jnp.zeros((8, BLK), f32)
    soft_sum = none
    for group in range(tiles // 8):
        parts = [
            three_parts(rows_scr[(group * K + k) * 8 : (group * K + k + 1) * 8, :]) for k in range(K)
        ]
        acc = jnp.zeros((32, 2 * TILE), f32)
        for q in range(4):
            keep = line % 4 == q
            lhs = [
                jnp.concatenate([jnp.where(keep, p, 0.0) for p in parts[k]] + [none], axis=0)
                for k in range(K)
            ]
            lhs = jnp.concatenate(lhs, axis=1).astype(bf16)
            acc += jnp.dot(lhs, inc_pair(group, q), preferred_element_type=f32)
        here = slice(group * 8, group * 8 + 8)
        both = acc[:8] + acc[8:16] + acc[16:24]
        priced = jnp.where(line < 4, both[:, :TILE], both[:, TILE:])
        reduced = cost_ref[here, :].astype(f32) - priced
        scaled = reduced / 8.0
        primal = 1.0 / (1.0 + jnp.exp(scaled))
        soft_sum += -8.0 * (jnp.maximum(-scaled, 0.0) + jnp.log1p(jnp.exp(-jnp.abs(scaled))))
        mean = primal if prev is None else 0.3 * primal + 0.7 * prev[here, :]
        mean_ref[here, :] = mean
        for s, p in enumerate(three_parts(mean)):
            parts_scr[pl.ds(group * 64 + s, 4, stride=8), :] = p[:4]
            parts_scr[pl.ds(group * 64 + 35 + s, 4, stride=8), :] = p[4:]
        for q in range(4):
            at = group * 64 + q * 8
            lhs = [parts_scr[at : at + 8, :], parts_scr[at + 32 : at + 40, :]]
            out = lax.dot_general(
                jnp.concatenate(lhs, axis=1).astype(bf16),
                inc_pair(group, q),
                (((1,), (1,)), ((), ())),
                preferred_element_type=f32,
            )
            for row, t in ((0, group * 8 + q), (3, group * 8 + q + 4)):
                part = out[row : row + 1] + out[row + 1 : row + 2] + out[row + 2 : row + 3]
                for k in range(K):
                    cover_scr[pl.ds(ids_ref[k, t] ^ turn, 1), :] += part[:, k * BLK : (k + 1) * BLK]
    soft_ref[...] = soft_sum
    mine_ref[...] = cover_scr[:half, :]
    send_ref[:half, :] = cover_scr[half:, :]
    send_ref[half:, :] = soft_sum


def first_kernel(
    ids_hbm, inc_hbm, cost_hbm, mult_hbm, inc_ref, mean_ref, soft_ref, mine_ref, send_ref, sum_ref,
    ids, raw, cost, mult, rows_scr, parts_scr, cover_scr, sems,
):
    tiles = cost.shape[0]
    small = [
        pltpu.make_async_copy(src, dst, sems.at[tiles + i])
        for i, (src, dst) in enumerate(((ids_hbm, ids), (mult_hbm, mult), (cost_hbm, cost)))
    ]
    large = [pltpu.make_async_copy(inc_hbm.at[t], raw.at[t], sems.at[t]) for t in range(tiles)]
    for copy in small:
        copy.start()
    for group in range(0, tiles, 8):
        for q in range(4):
            large[group + q].start()
            large[group + q + 4].start()
    for copy in small:
        copy.wait()
    seen = set()

    def inc_pair(group, q):
        pair = group * 4 + q
        if pair not in seen:
            seen.add(pair)
            for side in range(2):
                t = group * 8 + side * 4 + q
                large[t].wait()
                inc_ref[pair, :, side * TILE : (side + 1) * TILE] = (
                    raw[t].reshape(K * BLK, TILE).astype(f32).astype(inc_ref.dtype)
                )
        return inc_ref[pair]

    column_step(
        mult, ids, cost, inc_pair, None,
        rows_scr, parts_scr, cover_scr, mean_ref, soft_ref, mine_ref, send_ref,
    )
    sum_ref[...] = total_of(mult[...])


def total_of(v):
    n = v.shape[0] // 8
    v = v.reshape(n, 8, BLK)
    chains = [v[i] for i in range(4)]
    for i in range(4, n):
        chains[i % 4] = chains[i % 4] + v[i]
    return (chains[0] + chains[1]) + (chains[2] + chains[3])


def row_step(own_ref, other_ref, soft_ref, mult_ref, sum_ref, upper_ref, new_ref):
    me = my_core()
    half = mult_ref.shape[0] // 2
    slopes = [1.0 - ref[...].reshape(half, BLK) for ref in (own_ref, other_ref)]
    norm = total_of(slopes[0] * slopes[0]) + total_of(slopes[1] * slopes[1])
    value = jnp.sum(soft_ref[...] + sum_ref[...], keepdims=True)
    size = (upper_ref[0] - value) / (jnp.sum(norm, keepdims=True) + 1e-06)
    for slope, core in zip(slopes, (me, 1 - me)):
        at = pl.ds(pl.multiple_of(core * half, half), half)
        new_ref[at, :] = jnp.maximum(0.0, mult_ref[at, :] + size * slope)


def next_kernel(
    own_ref, other_ref, all_ref, mult_ref, sum_ref, upper_ref, ids_any, inc_ref, cost_ref, prev_ref,
    new_ref, mean_ref, soft_ref, mine_ref, send_ref, total_ref,
    ids, rows_scr, parts_scr, cover_scr, sem,
):
    copy = pltpu.make_async_copy(ids_any, ids, sem)
    copy.start()
    row_step(own_ref, other_ref, all_ref, mult_ref, sum_ref, upper_ref, new_ref)
    copy.wait()
    column_step(
        new_ref, ids, cost_ref, lambda group, q: inc_ref[group * 4 + q], prev_ref,
        rows_scr, parts_scr, cover_scr, mean_ref, soft_ref, mine_ref, send_ref,
    )
    total_ref[...] = total_of(new_ref[...])


def last_kernel(own_ref, other_ref, all_ref, mult_ref, sum_ref, upper_ref, mean_ref, new_ref, out_ref):
    out_ref[...] = mean_ref[...]
    row_step(own_ref, other_ref, all_ref, mult_ref, sum_ref, upper_ref, new_ref)


def pair_kernel(mine_ref, soft_ref, got_ref, out_ref):
    half = mine_ref.shape[0]
    out_ref[:, :OWN, :] = (mine_ref[...] + got_ref[:half, :]).reshape(NEAR, OWN, BLK)
    soft = soft_ref[...] + got_ref[half:, :]
    for i in range(NEAR):
        out_ref[i, OWN:, :] = soft


def sum_of(ref):
    parts = [ref[i] for i in range(ref.shape[0])]
    while len(parts) > 1:
        parts = [a + b for a, b in zip(parts[::2], parts[1::2])]
    return parts[0]


def owner_kernel(in_ref, out_ref):
    total = sum_of(in_ref)
    for i in range(FAR):
        out_ref[i] = total


def spread_kernel(in_ref, out_ref, soft_ref):
    total = sum_of(in_ref)
    for i in range(NEAR):
        out_ref[i] = total[:OWN]
    soft_ref[...] = total[OWN:]


def call(kernel, name, out, specs, scratch=(), mib=8):
    return pl.pallas_call(
        kernel,
        out_shape=out,
        in_specs=specs,
        out_specs=jax.tree.map(lambda _: VMEM, out),
        scratch_shapes=scratch,
        compiler_params=pltpu.CompilerParams(vmem_limit_bytes=mib << 20),
        name=name,
    )


def exchange(blocks, groups):
    return lax.all_to_all(blocks, "d", 0, 0, tiled=True, axis_index_groups=groups)


def local(block_ids, incidence, costs, start_mult, upper):
    tiles, rows = block_ids.shape[0], start_mult.shape[0]
    half = rows // 2
    ids = block_ids.T

    def floats(*shape):
        return jax.ShapeDtypeStruct((*shape, BLK), f32)

    outs = (floats(tiles), floats(8), floats(half), floats(half + 8), floats(8))
    scratch = [pltpu.VMEM((n, BLK), f32) for n in (tiles * K, tiles * 8, rows)]
    inc, mean, soft, mine, send, total = call(
        first_kernel,
        "first",
        (jax.ShapeDtypeStruct((tiles // 2, K * BLK, 2 * TILE), INC), *outs),
        [HBM] * 4,
        [
            pltpu.SMEM((K, tiles), jnp.int32),
            pltpu.VMEM((tiles, K, BLK, TILE), jnp.int32),
            pltpu.VMEM((tiles, TILE), jnp.int32),
            pltpu.VMEM((rows, BLK), f32),
            *scratch,
            pltpu.SemaphoreType.DMA((tiles + 3,)),
        ],
        mib=16,
    )(*(pltpu.with_memory_space_constraint(a, pltpu.HBM) for a in (ids, incidence, costs, start_mult)))
    mult = start_mult
    for step in range(ITERS):
        got = lax.ppermute(send, "d", SWAP)
        there = call(pair_kernel, "pair", floats(NEAR, SLOT), [VMEM] * 3)(mine, soft, got)
        there = exchange(there, PLANES)
        there = call(owner_kernel, "owner", floats(FAR, SLOT), [VMEM])(there)
        there = exchange(there, LINES)
        there, soft = call(spread_kernel, "spread", (floats(NEAR, OWN), floats(8)), [VMEM])(there)
        own = exchange(there, PLANES)
        other = lax.ppermute(own, "d", SWAP)
        rows_in = (own, other, soft, mult, total, upper)
        if step < ITERS - 1:
            mult, mean, soft, mine, send, total = call(
                next_kernel,
                "next",
                (floats(rows), *outs),
                [VMEM] * 5 + [SMEM, ANY] + [VMEM] * 3,
                [pltpu.SMEM((K, tiles), jnp.int32), *scratch, pltpu.SemaphoreType.DMA],
            )(*rows_in, ids, inc, costs, mean)
    return call(last_kernel, "last", (floats(rows), floats(tiles)), [VMEM] * 5 + [SMEM, VMEM])(*rows_in, mean)


def solution(mesh):
    return jax.shard_map(
        local,
        mesh=Mesh(mesh.devices.reshape(-1), ("d",)),
        in_specs=(
            P("d", None),
            P("d", None, None, None),
            P("d", None),
            P(),
            P(),
        ),
        out_specs=(P(), P("d", None)),
        check_vma=False,
    )
```

time: 130 us -> 124 us (0.954)
  blocking collectives: 108 us -> 93.3 us
  starting transfers between devices: 9.39 us -> 15.8 us
  waiting for transfers between devices: 2.56 us -> 5.28 us
    all_to_all x9, blocking collectives: 108 us -> 93.3 us  [exchange(): lax.all_to_all(blocks, 'd', 0, 0, tiled=True, axis_index_groups=groups)]
    ppermute x3 -> x6, starting transfers between devices: 9.39 us -> 15.8 us  [the longest x3 11.6 us: local(): other = lax.ppermute(own, 'd', SWAP)]
    ppermute x3 -> x6, waiting for transfers between devices: 2.56 us -> 5.28 us  [the longest x3 2.97 us: local(): got = lax.ppermute(send, 'd', SWAP)]
    pallas_call x10 -> x13, Pallas kernels: 7.87 us -> 7.52 us  [the longest x1 3.35 us: local(): call(first_kernel, 'first', (jax.ShapeDtypeStruct((tiles // 2, K * BLK, 2...]
  transfers between devices with their start and end apart: 3 -> 6, of which waited for: 3 -> 6; matrix products, arithmetic and copies ran while one was open for 0% -> 0% of each run, Pallas kernels for 0% -> 0%
where the time goes in v5:
time: 124 us; the launch traced here: 123 us
  blocking collectives  93.3 us (75%)
  starting transfers between devices  15.8 us (13%)
  Pallas kernels  7.52 us (6%)
  waiting for transfers between devices  5.28 us (4%)
  between operations  1.37 us (1%)
    all_to_all x9, blocking collectives, exchange(): lax.all_to_all(blocks, 'd', 0, 0, tiled=True, axis_index_groups=groups)  93.3 us
    ppermute x3, starting transfers between devices, local(): other = lax.ppermute(own, 'd', SWAP)  11.6 us
    ppermute x3, starting transfers between devices, local(): got = lax.ppermute(send, 'd', SWAP)  4.2 us
    pallas_call x1, Pallas kernels, local(): call(first_kernel, 'first', (jax.ShapeDtypeStruct((tiles // 2, K * BLK, 2...  3.35 us
    pallas_call x2, Pallas kernels, local(): call(next_kernel, 'next', (floats(rows), *outs), [VMEM] * 5 + [SMEM, ANY]...  3.1 us
    ppermute x3, waiting for transfers between devices, local(): got = lax.ppermute(send, 'd', SWAP)  2.97 us
  transfers between devices with their start and end apart: 6, of which 6 were waited for; matrix products, arithmetic and copies ran while one was open for 0% of the time, Pallas kernels for 0%

profile of v5, /device:TPU:1, one launch (start us, length us, event | category | flops | bytes accessed | tf_op | source)
XLA Modules:
  0.0 123.3 jit_solution(5225133114238542357)
XLA Ops:
  0.6 0.0 copy-start.1
  0.6 0.0 copy-start
  0.7 0.0 copy-start.2
  0.7 3.4 %first.1 = (f8e4m3fn[8,512,256]{2,1,0:T(32,128)(4,1)S(1)}, f32[16,128]{1,0:T(8,128)S(1)}, f32[8,128]{1,0:T(8,128)S(1)}, f32[256,128]{1,0:T(8,128)S(1)}, f32[264,128]{1,0:T(8,128)S(1)}, /*index=5*/f32[8,128]{1,0:T(8,128)S(1)}) custom-call(s32[4,16]{1,0:T(4,128)} %bitcast.1, s32[16,4,128,128]{3,2,1,0:T(8,128)} %inc_hbm.1, s32[16,128]{1,0:T(8,128)} %cost_ref.3, ...), custom_call_target="tpu_custom_call" | custom-call | tf_op jit(solution)/shard_map/first/pallas_call | solution.py:251
  4.0 3.3 %collective-permute-start = (f32[264,128]{1,0:T(8,128)S(1)}, f32[264,128]{1,0:T(8,128)S(1)}, u32[]{:S(2)}, u32[]{:S(2)}) collective-permute-start(f32[264,128]{1,0:T(8,128)S(1)} %get-tuple-element.28), channel_id=1, source_target_pairs={{0,32},{1,33},{2,34},{3,35},{4,36},{5,37},{6,38},{7,39},{8,40},{9,... | collective-permute-start | bytes 405512 | tf_op jit(solution)/shard_map/ppermute | solution.py:268
  7.3 1.0 collective-permute-done.got_ref
  8.3 10.4 %all_to_all.45.in_ref = f32[16,24,128]{2,1,0:T(8,128)S(1)} all-to-all(f32[16,24,128]{2,1,0:T(8,128)S(1)} %pair.3), channel_id=1, replica_groups={{80,144,16,8,216,152,24,0,208,64,88,200,136,72,128,192},{81,145,17,9,21..., dimensions={0} | all-to-all | bytes 393216 | tf_op jit(solution)/shard_map/all_to_all | solution.py:238
  18.7 14.8 %all_to_all.46.in_ref = f32[8,24,128]{2,1,0:T(8,128)S(1)} all-to-all(f32[8,24,128]{2,1,0:T(8,128)S(1)} %owner.3), channel_id=1, replica_groups={{0,2,4,6,7,1,3,5},{8,10,12,14,15,9,11,13},{16,18,20,22,23,17,19,21},{24..., dimensions={0} | all-to-all | bytes 196608 | tf_op jit(solution)/shard_map/all_to_all | solution.py:238
  33.5 10.0 %all_to_all.47.own_ref = f32[16,16,128]{2,1,0:T(8,128)S(1)} all-to-all(f32[16,16,128]{2,1,0:T(8,128)S(1)} %get-tuple-element.29), channel_id=1, replica_groups={{80,144,16,8,216,152,24,0,208,64,88,200,136,72,128,192},{81,145,17,9,21..., dimensions={0} | all-to-all | bytes 262144 | tf_op jit(solution)/shard_map/all_to_all | solution.py:238
  43.5 3.9 %collective-permute-start.1 = (f32[16,16,128]{2,1,0:T(8,128)S(1)}, f32[16,16,128]{2,1,0:T(8,128)S(1)}, u32[]{:S(2)}, u32[]{:S(2)}) collective-permute-start(f32[16,16,128]{2,1,0:T(8,128)S(1)} %all_to_all.47.own_ref), channel_id=1, source_target_pairs={{0,32},{1,33},{2,34},{3,35},{4,36},{5,37},{6,38},{7,39},{8,40},{9,... | collective-permute-start | bytes 393224 | tf_op jit(solution)/shard_map/ppermute | solution.py:275
  48.1 0.3 collective-permute-done.1.other_ref
  48.4 0.0 copy-done.1
  48.4 0.0 copy-done
  48.4 0.0 copy-done.2
  48.4 1.6 %next.2 = (f32[512,128]{1,0:T(8,128)S(1)}, f32[16,128]{1,0:T(8,128)S(1)}, f32[8,128]{1,0:T(8,128)S(1)}, f32[256,128]{1,0:T(8,128)S(1)}, f32[264,128]{1,0:T(8,128)S(1)}, /*index=5*/f32[8,128]{1,0:T(8,128)S(1)}) custom-call(f32[16,16,128]{2,1,0:T(8,128)S(1)} %all_to_all.47.own_ref, f32[16,16,128]{2,1,0:T(8,128)S(1)} %collective-permute-done.1.other_ref, ...), custom_call_target="tpu_custom_call" | custom-call | tf_op jit(solution)/shard_map/next/pallas_call | solution.py:278
  50.0 0.5 collective-permute-start.2
  50.4 1.0 collective-permute-done.2.got_ref
  51.5 10.1 %all_to_all.48.in_ref = f32[16,24,128]{2,1,0:T(8,128)S(1)} all-to-all(f32[16,24,128]{2,1,0:T(8,128)S(1)} %pair.4), channel_id=1, replica_groups={{80,144,16,8,216,152,24,0,208,64,88,200,136,72,128,192},{81,145,17,9,21..., dimensions={0} | all-to-all | bytes 393216 | tf_op jit(solution)/shard_map/all_to_all | solution.py:238
  61.6 9.1 %all_to_all.49.in_ref = f32[8,24,128]{2,1,0:T(8,128)S(1)} all-to-all(f32[8,24,128]{2,1,0:T(8,128)S(1)} %owner.4), channel_id=1, replica_groups={{0,2,4,6,7,1,3,5},{8,10,12,14,15,9,11,13},{16,18,20,22,23,17,19,21},{24..., dimensions={0} | all-to-all | bytes 196608 | tf_op jit(solution)/shard_map/all_to_all | solution.py:238
  70.6 10.0 %all_to_all.50.own_ref = f32[16,16,128]{2,1,0:T(8,128)S(1)} all-to-all(f32[16,16,128]{2,1,0:T(8,128)S(1)} %get-tuple-element.37), channel_id=1, replica_groups={{80,144,16,8,216,152,24,0,208,64,88,200,136,72,128,192},{81,145,17,9,21..., dimensions={0} | all-to-all | bytes 262144 | tf_op jit(solution)/shard_map/all_to_all | solution.py:238
  80.6 3.9 %collective-permute-start.3 = (f32[16,16,128]{2,1,0:T(8,128)S(1)}, f32[16,16,128]{2,1,0:T(8,128)S(1)}, u32[]{:S(2)}, u32[]{:S(2)}) collective-permute-start(f32[16,16,128]{2,1,0:T(8,128)S(1)} %all_to_all.50.own_ref), channel_id=1, source_target_pairs={{0,32},{1,33},{2,34},{3,35},{4,36},{5,37},{6,38},{7,39},{8,40},{9,... | collective-permute-start | bytes 393224 | tf_op jit(solution)/shard_map/ppermute | solution.py:275
  84.4 1.0 collective-permute-done.3.other_ref
  85.4 1.6 %next.3 = (f32[512,128]{1,0:T(8,128)S(1)}, f32[16,128]{1,0:T(8,128)S(1)}, f32[8,128]{1,0:T(8,128)S(1)}, f32[256,128]{1,0:T(8,128)S(1)}, f32[264,128]{1,0:T(8,128)S(1)}, /*index=5*/f32[8,128]{1,0:T(8,128)S(1)}) custom-call(f32[16,16,128]{2,1,0:T(8,128)S(1)} %all_to_all.50.own_ref, f32[16,16,128]{2,1,0:T(8,128)S(1)} %collective-permute-done.3.other_ref, ...), custom_call_target="tpu_custom_call" | custom-call | tf_op jit(solution)/shard_map/next/pallas_call | solution.py:278
  87.0 0.4 collective-permute-start.4
  87.4 1.0 collective-permute-done.4.got_ref
  88.4 10.1 %all_to_all.51.in_ref = f32[16,24,128]{2,1,0:T(8,128)S(1)} all-to-all(f32[16,24,128]{2,1,0:T(8,128)S(1)} %pair.5), channel_id=1, replica_groups={{80,144,16,8,216,152,24,0,208,64,88,200,136,72,128,192},{81,145,17,9,21..., dimensions={0} | all-to-all | bytes 393216 | tf_op jit(solution)/shard_map/all_to_all | solution.py:238
  98.5 9.1 %all_to_all.52.in_ref = f32[8,24,128]{2,1,0:T(8,128)S(1)} all-to-all(f32[8,24,128]{2,1,0:T(8,128)S(1)} %owner.5), channel_id=1, replica_groups={{0,2,4,6,7,1,3,5},{8,10,12,14,15,9,11,13},{16,18,20,22,23,17,19,21},{24..., dimensions={0} | all-to-all | bytes 196608 | tf_op jit(solution)/shard_map/all_to_all | solution.py:238
  107.6 10.0 %all_to_all.53.own_ref = f32[16,16,128]{2,1,0:T(8,128)S(1)} all-to-all(f32[16,16,128]{2,1,0:T(8,128)S(1)} %get-tuple-element.45), channel_id=1, replica_groups={{80,144,16,8,216,152,24,0,208,64,88,200,136,72,128,192},{81,145,17,9,21..., dimensions={0} | all-to-all | bytes 262144 | tf_op jit(solution)/shard_map/all_to_all | solution.py:238
  117.6 3.9 %collective-permute-start.5 = (f32[16,16,128]{2,1,0:T(8,128)S(1)}, f32[16,16,128]{2,1,0:T(8,128)S(1)}, u32[]{:S(2)}, u32[]{:S(2)}) collective-permute-start(f32[16,16,128]{2,1,0:T(8,128)S(1)} %all_to_all.53.own_ref), channel_id=1, source_target_pairs={{0,32},{1,33},{2,34},{3,35},{4,36},{5,37},{6,38},{7,39},{8,40},{9,... | collective-permute-start | bytes 393224 | tf_op jit(solution)/shard_map/ppermute | solution.py:275
  121.4 1.0 collective-permute-done.5.other_ref
  122.4 0.9 last.1
  (9 shorter events, 0.2 us)
Async XLA Ops:
  0.6 47.8 %copy-start.1 = (s32[16,128]{1,0:T(8,128)S(1)}, s32[16,128]{1,0:T(8,128)}, u32[]{:S(2)}) copy-start(s32[16,128]{1,0:T(8,128)} %cost_ref.3) | copy-start | bytes 24580
  0.6 47.8 %copy-start = (f32[512,128]{1,0:T(8,128)S(1)}, f32[512,128]{1,0:T(8,128)}, u32[]{:S(2)}) copy-start(f32[512,128]{1,0:T(8,128)} %mult_ref.1) | copy-start | bytes 786436
  0.7 47.8 %copy-start.2 = (s32[16,4]{0,1:T(4,128)S(1)}, s32[16,4]{0,1:T(4,128)}, u32[]{:S(2)}) copy-start(s32[16,4]{0,1:T(4,128)} %param.5) | copy-start | bytes 772
  4.0 4.3 %collective-permute-start = (f32[264,128]{1,0:T(8,128)S(1)}, f32[264,128]{1,0:T(8,128)S(1)}, u32[]{:S(2)}, u32[]{:S(2)}) collective-permute-start(f32[264,128]{1,0:T(8,128)S(1)} %get-tuple-element.28), channel_id=1, source_target_pairs={{0,32},{1,33},{2,34},{3,35},{4,36},{5,37},{6,38},{7,39},{8,40},{9,... | collective-permute-start | bytes 405512 | tf_op jit(solution)/shard_map/ppermute | solution.py:268
  43.5 4.9 %collective-permute-start.1 = (f32[16,16,128]{2,1,0:T(8,128)S(1)}, f32[16,16,128]{2,1,0:T(8,128)S(1)}, u32[]{:S(2)}, u32[]{:S(2)}) collective-permute-start(f32[16,16,128]{2,1,0:T(8,128)S(1)} %all_to_all.47.own_ref), channel_id=1, source_target_pairs={{0,32},{1,33},{2,34},{3,35},{4,36},{5,37},{6,38},{7,39},{8,40},{9,... | collective-permute-start | bytes 393224 | tf_op jit(solution)/shard_map/ppermute | solution.py:275
  50.0 1.5 %collective-permute-start.2 = (f32[264,128]{1,0:T(8,128)S(1)}, f32[264,128]{1,0:T(8,128)S(1)}, u32[]{:S(2)}, u32[]{:S(2)}) collective-permute-start(f32[264,128]{1,0:T(8,128)S(1)} %get-tuple-element.36), channel_id=1, source_target_pairs={{0,32},{1,33},{2,34},{3,35},{4,36},{5,37},{6,38},{7,39},{8,40},{9,... | collective-permute-start | bytes 405512 | tf_op jit(solution)/shard_map/ppermute | solution.py:268
  80.6 4.8 %collective-permute-start.3 = (f32[16,16,128]{2,1,0:T(8,128)S(1)}, f32[16,16,128]{2,1,0:T(8,128)S(1)}, u32[]{:S(2)}, u32[]{:S(2)}) collective-permute-start(f32[16,16,128]{2,1,0:T(8,128)S(1)} %all_to_all.50.own_ref), channel_id=1, source_target_pairs={{0,32},{1,33},{2,34},{3,35},{4,36},{5,37},{6,38},{7,39},{8,40},{9,... | collective-permute-start | bytes 393224 | tf_op jit(solution)/shard_map/ppermute | solution.py:275
  87.0 1.4 %collective-permute-start.4 = (f32[264,128]{1,0:T(8,128)S(1)}, f32[264,128]{1,0:T(8,128)S(1)}, u32[]{:S(2)}, u32[]{:S(2)}) collective-permute-start(f32[264,128]{1,0:T(8,128)S(1)} %get-tuple-element.44), channel_id=1, source_target_pairs={{0,32},{1,33},{2,34},{3,35},{4,36},{5,37},{6,38},{7,39},{8,40},{9,... | collective-permute-start | bytes 405512 | tf_op jit(solution)/shard_map/ppermute | solution.py:268
  117.6 4.8 %collective-permute-start.5 = (f32[16,16,128]{2,1,0:T(8,128)S(1)}, f32[16,16,128]{2,1,0:T(8,128)S(1)}, u32[]{:S(2)}, u32[]{:S(2)}) collective-permute-start(f32[16,16,128]{2,1,0:T(8,128)S(1)} %all_to_all.53.own_ref), channel_id=1, source_target_pairs={{0,32},{1,33},{2,34},{3,35},{4,36},{5,37},{6,38},{7,39},{8,40},{9,... | collective-permute-start | bytes 393224 | tf_op jit(solution)/shard_map/ppermute | solution.py:275

commit v6 on v5

v6 whole, which is shorter than its diff:
```python
import jax
import jax.numpy as jnp
from jax import lax
from jax.experimental import pallas as pl
from jax.experimental.pallas import tpu as pltpu
from jax.sharding import Mesh
from jax.sharding import PartitionSpec as P

BLK = 128
TILE = 128
K = 4
ITERS = 3
X, C, Y, Z = 4, 2, 4, 8
NEAR, FAR = X * C * Y, Z
OWN = 16
SLOT = OWN + 1
PLANE_ORDER = (
    (2, 1, 1), (1, 1, 2), (1, 0, 2), (0, 1, 0), (0, 1, 1), (1, 0, 1), (3, 1, 1), (0, 0, 1),
    (3, 1, 3), (1, 1, 1), (3, 1, 2), (2, 0, 3), (3, 0, 2), (3, 0, 0), (3, 0, 3), (1, 0, 0),
    (0, 1, 3), (3, 0, 1), (2, 1, 3), (0, 0, 0), (2, 0, 2), (3, 1, 0), (0, 0, 3), (2, 1, 2),
    (0, 1, 2), (2, 1, 0), (1, 1, 3), (2, 0, 0), (1, 1, 0), (0, 0, 2), (2, 0, 1), (1, 0, 3),
)
LINE_ORDER = (0, 2, 4, 6, 7, 1, 3, 5)


def device(x, c, y, z):
    return ((x * C + c) * Y + y) * Z + z


PLANES = [[device(x, c, y, z) for x, c, y in PLANE_ORDER] for z in range(Z)]
LINES = [
    [device(x, c, y, z) for z in LINE_ORDER] for x in range(X) for c in range(C) for y in range(Y)
]

f32, bf16 = jnp.float32, jnp.bfloat16
INC = jnp.float8_e4m3fn
VMEM = pl.BlockSpec(memory_space=pltpu.VMEM)
ANY = pl.BlockSpec(memory_space=pl.ANY)
HBM = pl.BlockSpec(memory_space=pltpu.HBM)


def three_parts(v):
    high = v.astype(bf16).astype(f32)
    rest = v - high
    middle = rest.astype(bf16).astype(f32)
    return high, middle, rest - middle


def column_step(mult_ref, ids_ref, cost_ref, inc_pair, prev, rows_scr, parts_scr, mean_ref, soft_ref, cover_ref):
    tiles = cost_ref.shape[0]
    for t in range(tiles):
        for k in range(K):
            at = (t // 8 * K + k) * 8 + t % 8
            rows_scr[at : at + 1, :] = mult_ref[pl.ds(ids_ref[k, t], 1), :]
    parts_scr[...] = jnp.zeros_like(parts_scr)
    cover_ref[...] = jnp.zeros_like(cover_ref)
    line = lax.broadcasted_iota(jnp.int32, (8, BLK), 0)
    none = jnp.zeros((8, BLK), f32)
    soft_sum = none
    for group in range(tiles // 8):
        parts = [
            three_parts(rows_scr[(group * K + k) * 8 : (group * K + k + 1) * 8, :]) for k in range(K)
        ]
        acc = jnp.zeros((32, 2 * TILE), f32)
        for q in range(4):
            keep = line % 4 == q
            lhs = [
                jnp.concatenate([jnp.where(keep, p, 0.0) for p in parts[k]] + [none], axis=0)
                for k in range(K)
            ]
            lhs = jnp.concatenate(lhs, axis=1).astype(bf16)
            acc += jnp.dot(lhs, inc_pair(group, q), preferred_element_type=f32)
        here = slice(group * 8, group * 8 + 8)
        both = acc[:8] + acc[8:16] + acc[16:24]
        priced = jnp.where(line < 4, both[:, :TILE], both[:, TILE:])
        reduced = cost_ref[here, :].astype(f32) - priced
        scaled = reduced / 8.0
        primal = 1.0 / (1.0 + jnp.exp(scaled))
        soft_sum += -8.0 * (jnp.maximum(-scaled, 0.0) + jnp.log1p(jnp.exp(-jnp.abs(scaled))))
        mean = primal if prev is None else 0.3 * primal + 0.7 * prev[here, :]
        mean_ref[here, :] = mean
        for s, p in enumerate(three_parts(mean)):
            parts_scr[pl.ds(group * 64 + s, 4, stride=8), :] = p[:4]
            parts_scr[pl.ds(group * 64 + 35 + s, 4, stride=8), :] = p[4:]
        for q in range(4):
            at = group * 64 + q * 8
            lhs = [parts_scr[at : at + 8, :], parts_scr[at + 32 : at + 40, :]]
            out = lax.dot_general(
                jnp.concatenate(lhs, axis=1).astype(bf16),
                inc_pair(group, q),
                (((1,), (1,)), ((), ())),
                preferred_element_type=f32,
            )
            for row, t in ((0, group * 8 + q), (3, group * 8 + q + 4)):
                part = out[row : row + 1] + out[row + 1 : row + 2] + out[row + 2 : row + 3]
                for k in range(K):
                    cover_ref[pl.ds(ids_ref[k, t], 1), :] += part[:, k * BLK : (k + 1) * BLK]
    soft_ref[...] = soft_sum


def first_kernel(
    ids_hbm, inc_hbm, cost_hbm, mult_hbm, upper,
    inc_ref, mean_ref, soft_ref, cover_ref, sum_ref, upper_ref,
    ids, raw, cost, mult, rows_scr, parts_scr, sems,
):
    tiles = cost.shape[0]
    small = [
        pltpu.make_async_copy(src, dst, sems.at[tiles + i])
        for i, (src, dst) in enumerate(((ids_hbm, ids), (mult_hbm, mult), (cost_hbm, cost)))
    ]
    large = [pltpu.make_async_copy(inc_hbm.at[t], raw.at[t], sems.at[t]) for t in range(tiles)]
    for copy in small:
        copy.start()
    for group in range(0, tiles, 8):
        for q in range(4):
            large[group + q].start()
            large[group + q + 4].start()
    for copy in small:
        copy.wait()
    seen = set()

    def inc_pair(group, q):
        pair = group * 4 + q
        if pair not in seen:
            seen.add(pair)
            for side in range(2):
                t = group * 8 + side * 4 + q
                large[t].wait()
                inc_ref[pair, :, side * TILE : (side + 1) * TILE] = (
                    raw[t].reshape(K * BLK, TILE).astype(f32).astype(inc_ref.dtype)
                )
        return inc_ref[pair]

    column_step(mult, ids, cost, inc_pair, None, rows_scr, parts_scr, mean_ref, soft_ref, cover_ref)
    sum_ref[...] = total_of(mult[...])
    upper_ref[...] = jnp.full(upper_ref.shape, upper[0], f32)


def total_of(v):
    n = v.shape[0] // 8
    v = v.reshape(n, 8, BLK)
    chains = [v[i] for i in range(4)]
    for i in range(4, n):
        chains[i % 4] = chains[i % 4] + v[i]
    return (chains[0] + chains[1]) + (chains[2] + chains[3])


def row_step(gathered, mult_ref, sum_ref, upper_ref, new_ref):
    norm, soft = [], sum_ref[...]
    lines = []
    for i in range(NEAR):
        slope = 1.0 - gathered[i * SLOT : i * SLOT + OWN, :]
        norm.append(slope * slope)
        lines.append(gathered[i * SLOT + OWN : (i + 1) * SLOT, :])
    value = jnp.sum(soft, keepdims=True) + jnp.sum(tree_sum(lines), keepdims=True)
    size = (upper_ref[:1, :1] - value) / (jnp.sum(tree_sum(norm), keepdims=True) + 1e-06)
    for i in range(NEAR):
        slope = 1.0 - gathered[i * SLOT : i * SLOT + OWN, :]
        here = slice(i * OWN, (i + 1) * OWN)
        new_ref[here, :] = jnp.maximum(0.0, mult_ref[here, :] + size * slope)


def next_kernel(
    gathered, mult_ref, sum_ref, upper_ref, ids_any, inc_ref, cost_ref, prev_ref,
    new_ref, mean_ref, soft_ref, cover_ref, total_ref, ids, rows_scr, parts_scr, sem,
):
    copy = pltpu.make_async_copy(ids_any, ids, sem)
    copy.start()
    row_step(gathered, mult_ref, sum_ref, upper_ref, new_ref)
    copy.wait()
    column_step(
        new_ref, ids, cost_ref, lambda group, q: inc_ref[group * 4 + q],
        prev_ref, rows_scr, parts_scr, mean_ref, soft_ref, cover_ref,
    )
    total_ref[...] = total_of(new_ref[...])


def last_kernel(gathered, mult_ref, sum_ref, upper_ref, mean_ref, new_ref, out_ref):
    out_ref[...] = mean_ref[...]
    row_step(gathered, mult_ref, sum_ref, upper_ref, new_ref)


def tree_sum(parts):
    while len(parts) > 1:
        parts = [a + b for a, b in zip(parts[::2], parts[1::2])]
    return parts[0]


def owner_kernel(in_ref, soft_ref, out_ref):
    total = tree_sum([in_ref[i] for i in range(NEAR)])
    soft = jnp.sum(soft_ref[...], axis=0, keepdims=True)
    for i in range(FAR):
        out_ref[i * SLOT : i * SLOT + OWN, :] = total
        out_ref[i * SLOT + OWN : (i + 1) * SLOT, :] = soft


def spread_kernel(in_ref, out_ref):
    total = tree_sum([in_ref[i * SLOT : i * SLOT + OWN, :] for i in range(FAR)])
    soft = tree_sum([in_ref[i * SLOT + OWN : (i + 1) * SLOT, :] for i in range(FAR)])
    for i in range(NEAR):
        out_ref[i * SLOT : i * SLOT + OWN, :] = total
        out_ref[i * SLOT + OWN : (i + 1) * SLOT, :] = soft


def call(kernel, name, out, specs, scratch=(), mib=8):
    return pl.pallas_call(
        kernel,
        out_shape=out,
        in_specs=specs,
        out_specs=jax.tree.map(lambda _: VMEM, out),
        scratch_shapes=scratch,
        compiler_params=pltpu.CompilerParams(vmem_limit_bytes=mib << 20),
        name=name,
    )


def exchange(blocks, groups):
    shape = blocks.shape
    blocks = blocks.reshape(len(groups[0]), -1)
    return lax.all_to_all(blocks, "d", 0, 0, tiled=True, axis_index_groups=groups).reshape(shape)


def local(block_ids, incidence, costs, start_mult, upper):
    tiles, rows = block_ids.shape[0], start_mult.shape[0]
    ids = block_ids.T

    def floats(*shape):
        return jax.ShapeDtypeStruct((*shape, BLK), f32)

    outs = (floats(tiles), floats(8), floats(rows), floats(8))
    scratch = [pltpu.VMEM((n, BLK), f32) for n in (tiles * K, tiles * 8)]
    inc, mean, soft, cover, total, top = call(
        first_kernel,
        "first",
        (jax.ShapeDtypeStruct((tiles // 2, K * BLK, 2 * TILE), INC), *outs, floats(8)),
        [HBM] * 4 + [pl.BlockSpec(memory_space=pltpu.SMEM)],
        [
            pltpu.SMEM((K, tiles), jnp.int32),
            pltpu.VMEM((tiles, K, BLK, TILE), jnp.int32),
            pltpu.VMEM((tiles, TILE), jnp.int32),
            pltpu.VMEM((rows, BLK), f32),
            *scratch,
            pltpu.SemaphoreType.DMA((tiles + 3,)),
        ],
        mib=16,
    )(*(pltpu.with_memory_space_constraint(a, pltpu.HBM) for a in (ids, incidence, costs, start_mult)), upper)
    mult = start_mult
    for step in range(ITERS):
        there = lax.all_to_all(
            cover.reshape(NEAR, OWN, BLK), "d", 0, 0, tiled=True, axis_index_groups=PLANES
        )
        there = call(owner_kernel, "owner", floats(FAR * SLOT), [VMEM] * 2)(there, soft)
        there = exchange(there, LINES)
        there = call(spread_kernel, "spread", floats(NEAR * SLOT), [VMEM])(there)
        rows_in = (exchange(there, PLANES), mult, total, top)
        if step < ITERS - 1:
            mult, mean, soft, cover, total = call(
                next_kernel,
                "next",
                (floats(rows), *outs),
                [VMEM] * 4 + [ANY] + [VMEM] * 3,
                [pltpu.SMEM((K, tiles), jnp.int32), *scratch, pltpu.SemaphoreType.DMA],
            )(*rows_in, ids, inc, costs, mean)
    return call(last_kernel, "last", (floats(rows), floats(tiles)), [VMEM] * 5)(*rows_in, mean)


def solution(mesh):
    return jax.shard_map(
        local,
        mesh=Mesh(mesh.devices.reshape(-1), ("d",)),
        in_specs=(
            P("d", None),
            P("d", None, None, None),
            P("d", None),
            P(),
            P(),
        ),
        out_specs=(P(), P("d", None)),
        check_vma=False,
    )
```

time: 124 us -> 121 us (0.976)
  blocking collectives: 93.3 us -> 112 us
  starting transfers between devices: 15.8 us -> 0 us
  waiting for transfers between devices: 5.28 us -> 0 us
    all_to_all x0 -> x3, blocking collectives: none -> 39.2 us  [local(): lax.all_to_all(cover.reshape(NEAR, OWN, BLK), 'd', 0, 0, tiled=True, axis...]
    all_to_all x9 -> x6, blocking collectives: 93.3 us -> 72.4 us  [exchange(): lax.all_to_all(blocks, 'd', 0, 0, tiled=True, axis_index_groups=groups)]
    ppermute x6 -> x0, starting transfers between devices: 15.8 us -> none  [the longest x3 11.6 us: local(): other = lax.ppermute(own, 'd', SWAP)]
    ppermute x6 -> x0, waiting for transfers between devices: 5.28 us -> none  [the longest x3 2.97 us: local(): got = lax.ppermute(send, 'd', SWAP)]
    pallas_call x12 -> x9, Pallas kernels: 4.16 us -> 4.18 us  [the longest x2 3.08 us: local(): call(next_kernel, 'next', (floats(rows), *outs), [VMEM] * 4 + [ANY] + [VM...]
  transfers between devices with their start and end apart: 6 -> 0, of which waited for: 6 -> 0; matrix products, arithmetic and copies ran while one was open for 0% -> 0% of each run, Pallas kernels for 0% -> 0%
where the time goes in v6:
time: 121 us; the launch traced here: 120 us
  blocking collectives  112 us (93%)
  Pallas kernels  7.47 us (6%)
  between operations  1.4 us (1%)
    all_to_all x6, blocking collectives, exchange(): lax.all_to_all(blocks, 'd', 0, 0, tiled=True, axis_index_groups=groups)  72.4 us
    all_to_all x3, blocking collectives, local(): lax.all_to_all(cover.reshape(NEAR, OWN, BLK), 'd', 0, 0, tiled=True, axis...  39.2 us
    pallas_call x1, Pallas kernels, local(): call(first_kernel, 'first', (jax.ShapeDtypeStruct((tiles // 2, K * BLK, 2...  3.3 us
    pallas_call x2, Pallas kernels, local(): call(next_kernel, 'next', (floats(rows), *outs), [VMEM] * 4 + [ANY] + [VM...  3.08 us

profile of v6, /device:TPU:1, one launch (start us, length us, event | category | flops | bytes accessed | tf_op | source)
XLA Modules:
  0.0 120.5 jit_solution(14547020533428522434)
XLA Ops:
  0.6 0.0 copy-start.1
  0.6 0.0 copy-start
  0.7 0.0 copy-start.2
  1.3 3.3 %first.1 = (f8e4m3fn[8,512,256]{2,1,0:T(32,128)(4,1)S(1)}, f32[16,128]{1,0:T(8,128)S(1)}, f32[8,128]{1,0:T(8,128)S(1)}, f32[512,128]{1,0:T(8,128)S(1)}, f32[8,128]{1,0:T(8,128)S(1)}, /*index=5*/f32[8,128]{1,0:T(8,128)S(1)}) custom-call(s32[4,16]{1,0:T(4,128)} %bitcast.31, s32[16,4,128,128]{3,2,1,0:T(8,128)} %inc_hbm.1, s32[16,128]{1,0:T(8,128)} %cost_ref.3, ...), custom_call_target="tpu_custom_call" | custom-call | tf_op jit(solution)/shard_map/first/pallas_call | solution.py:232
  4.7 15.5 %all_to_all.69.in_ref = f32[32,16,128]{2,1,0:T(8,128)S(1)} all-to-all(f32[32,16,128]{2,1,0:T(8,128)S(1)} %bitcast.30), channel_id=1, replica_groups={{168,112,80,32,40,72,232,8,248,104,240,152,208,192,216,64,56,200,184,0,..., dimensions={0} | all-to-all | bytes 524288 | tf_op jit(solution)/shard_map/all_to_all | solution.py:249
  20.2 14.8 %all_to_all.70 = f32[8,1,2176]{2,1,0:T(1,128)S(1)} all-to-all(f32[8,1,2176]{2,1,0:T(1,128)S(1)} %bitcast.22), channel_id=1, replica_groups={{0,2,4,6,7,1,3,5},{8,10,12,14,15,9,11,13},{16,18,20,22,23,17,19,21},{24..., dimensions={0} | all-to-all | bytes 139264 | tf_op jit(solution)/shard_map/all_to_all | solution.py:220
  35.0 13.2 %all_to_all.71 = f32[32,1,2176]{2,1,0:T(1,128)S(1)} all-to-all(f32[32,1,2176]{2,1,0:T(1,128)S(1)} %bitcast.19), channel_id=1, replica_groups={{168,112,80,32,40,72,232,8,248,104,240,152,208,192,216,64,56,200,184,0,..., dimensions={0} | all-to-all | bytes 557056 | tf_op jit(solution)/shard_map/all_to_all | solution.py:220
  48.2 0.0 copy-done.1
  48.2 0.0 copy-done
  48.2 0.0 copy-done.2
  48.2 1.5 %next.2 = (f32[512,128]{1,0:T(8,128)S(1)}, f32[16,128]{1,0:T(8,128)S(1)}, f32[8,128]{1,0:T(8,128)S(1)}, f32[512,128]{1,0:T(8,128)S(1)}, f32[8,128]{1,0:T(8,128)S(1)}) custom-call(f32[544,128]{1,0:T(8,128)S(1)} %bitcast.17, f32[512,128]{1,0:T(8,128)S(1)} %copy-done, f32[8,128]{1,0:T(8,128)S(1)} %get-tuple-element.20.sum_ref, ...), custom_call_target="tpu_custom_call" | custom-call | tf_op jit(solution)/shard_map/next/pallas_call | solution.py:257
  49.8 11.8 %all_to_all.72.in_ref = f32[32,16,128]{2,1,0:T(8,128)S(1)} all-to-all(f32[32,16,128]{2,1,0:T(8,128)S(1)} %bitcast.29), channel_id=1, replica_groups={{168,112,80,32,40,72,232,8,248,104,240,152,208,192,216,64,56,200,184,0,..., dimensions={0} | all-to-all | bytes 524288 | tf_op jit(solution)/shard_map/all_to_all | solution.py:249
  61.7 9.1 %all_to_all.73 = f32[8,1,2176]{2,1,0:T(1,128)S(1)} all-to-all(f32[8,1,2176]{2,1,0:T(1,128)S(1)} %bitcast.23), channel_id=1, replica_groups={{0,2,4,6,7,1,3,5},{8,10,12,14,15,9,11,13},{16,18,20,22,23,17,19,21},{24..., dimensions={0} | all-to-all | bytes 139264 | tf_op jit(solution)/shard_map/all_to_all | solution.py:220
  70.8 13.0 %all_to_all.74 = f32[32,1,2176]{2,1,0:T(1,128)S(1)} all-to-all(f32[32,1,2176]{2,1,0:T(1,128)S(1)} %bitcast.20), channel_id=1, replica_groups={{168,112,80,32,40,72,232,8,248,104,240,152,208,192,216,64,56,200,184,0,..., dimensions={0} | all-to-all | bytes 557056 | tf_op jit(solution)/shard_map/all_to_all | solution.py:220
  83.9 1.5 %next.3 = (f32[512,128]{1,0:T(8,128)S(1)}, f32[16,128]{1,0:T(8,128)S(1)}, f32[8,128]{1,0:T(8,128)S(1)}, f32[512,128]{1,0:T(8,128)S(1)}, f32[8,128]{1,0:T(8,128)S(1)}) custom-call(f32[544,128]{1,0:T(8,128)S(1)} %bitcast.16, f32[512,128]{1,0:T(8,128)S(1)} %get-tuple-element.26.mult_ref, f32[8,128]{1,0:T(8,128)S(1)} %get-tuple-element.27.sum_ref, ...), custom_call_target="tpu_custom_call" | custom-call | tf_op jit(solution)/shard_map/next/pallas_call | solution.py:257
  85.4 11.8 %all_to_all.75.in_ref = f32[32,16,128]{2,1,0:T(8,128)S(1)} all-to-all(f32[32,16,128]{2,1,0:T(8,128)S(1)} %bitcast.28), channel_id=1, replica_groups={{168,112,80,32,40,72,232,8,248,104,240,152,208,192,216,64,56,200,184,0,..., dimensions={0} | all-to-all | bytes 524288 | tf_op jit(solution)/shard_map/all_to_all | solution.py:249
  97.3 9.1 %all_to_all.76 = f32[8,1,2176]{2,1,0:T(1,128)S(1)} all-to-all(f32[8,1,2176]{2,1,0:T(1,128)S(1)} %bitcast.24), channel_id=1, replica_groups={{0,2,4,6,7,1,3,5},{8,10,12,14,15,9,11,13},{16,18,20,22,23,17,19,21},{24..., dimensions={0} | all-to-all | bytes 139264 | tf_op jit(solution)/shard_map/all_to_all | solution.py:220
  106.5 13.0 %all_to_all.77 = f32[32,1,2176]{2,1,0:T(1,128)S(1)} all-to-all(f32[32,1,2176]{2,1,0:T(1,128)S(1)} %bitcast.21), channel_id=1, replica_groups={{168,112,80,32,40,72,232,8,248,104,240,152,208,192,216,64,56,200,184,0,..., dimensions={0} | all-to-all | bytes 557056 | tf_op jit(solution)/shard_map/all_to_all | solution.py:220
  119.5 0.9 last.1
  (6 shorter events, 0.2 us)
Async XLA Ops:
  0.6 47.6 %copy-start.1 = (s32[16,128]{1,0:T(8,128)S(1)}, s32[16,128]{1,0:T(8,128)}, u32[]{:S(2)}) copy-start(s32[16,128]{1,0:T(8,128)} %cost_ref.3) | copy-start | bytes 24580
  0.6 47.6 %copy-start = (f32[512,128]{1,0:T(8,128)S(1)}, f32[512,128]{1,0:T(8,128)}, u32[]{:S(2)}) copy-start(f32[512,128]{1,0:T(8,128)} %mult_ref.1) | copy-start | bytes 786436
  0.7 47.6 %copy-start.2 = (s32[16,4]{0,1:T(4,128)S(1)}, s32[16,4]{0,1:T(4,128)}, u32[]{:S(2)}) copy-start(s32[16,4]{0,1:T(4,128)} %param.5) | copy-start | bytes 772

commit v7 on v6

--- a/solution.py
+++ b/solution.py
@@ -15,21 +15,21 @@
 OWN = 16
 SLOT = OWN + 1
 PLANE_ORDER = (
-    (2, 1, 1), (1, 1, 2), (1, 0, 2), (0, 1, 0), (0, 1, 1), (1, 0, 1), (3, 1, 1), (0, 0, 1),
-    (3, 1, 3), (1, 1, 1), (3, 1, 2), (2, 0, 3), (3, 0, 2), (3, 0, 0), (3, 0, 3), (1, 0, 0),
-    (0, 1, 3), (3, 0, 1), (2, 1, 3), (0, 0, 0), (2, 0, 2), (3, 1, 0), (0, 0, 3), (2, 1, 2),
-    (0, 1, 2), (2, 1, 0), (1, 1, 3), (2, 0, 0), (1, 1, 0), (0, 0, 2), (2, 0, 1), (1, 0, 3),
+    (1, 0, 2), (1, 1, 1), (3, 0, 3), (3, 1, 2), (2, 1, 1), (0, 1, 3), (0, 0, 1), (3, 0, 0),
+    (2, 0, 3), (1, 0, 3), (0, 1, 2), (0, 1, 0), (1, 0, 0), (2, 1, 0), (3, 1, 1), (2, 0, 2),
+    (1, 1, 2), (1, 0, 1), (3, 1, 3), (3, 0, 2), (2, 0, 1), (0, 0, 3), (0, 1, 1), (3, 1, 0),
+    (2, 1, 3), (1, 1, 3), (0, 0, 2), (0, 0, 0), (1, 1, 0), (2, 0, 0), (3, 0, 1), (2, 1, 2),
 )
-LINE_ORDER = (0, 2, 4, 6, 7, 1, 3, 5)
+LINE_ORDER = (6, 0, 3, 2, 5, 1, 4, 7)
 
 
 def device(x, c, y, z):
     return ((x * C + c) * Y + y) * Z + z
 
 
-PLANES = [[device(x, c, y, z) for x, c, y in PLANE_ORDER] for z in range(Z)]
+PLANES = [[device(x, c ^ (z >> 2), y, z) for x, c, y in PLANE_ORDER] for z in range(Z)]
 LINES = [
-    [device(x, c, y, z) for z in LINE_ORDER] for x in range(X) for c in range(C) for y in range(Y)
+    [device(x, c ^ (z >> 2), y, z) for z in LINE_ORDER] for x in range(X) for c in range(C) for y in range(Y)
 ]
 
 f32, bf16 = jnp.float32, jnp.bfloat16

time: 121 us -> 117 us (0.967)
  blocking collectives: 112 us -> 107 us
    all_to_all x6, blocking collectives: 72.4 us -> 68.7 us  [exchange(): lax.all_to_all(blocks, 'd', 0, 0, tiled=True, axis_index_groups=groups)]
where the time goes in v7:
time: 117 us; the launch traced here: 116 us
  blocking collectives  107 us (91%)
  Pallas kernels  7.47 us (6%)
  between operations  1.4 us (1%)
    all_to_all x6, blocking collectives, exchange(): lax.all_to_all(blocks, 'd', 0, 0, tiled=True, axis_index_groups=groups)  68.7 us
    all_to_all x3, blocking collectives, local(): lax.all_to_all(cover.reshape(NEAR, OWN, BLK), 'd', 0, 0, tiled=True, axis...  38.7 us
    pallas_call x1, Pallas kernels, local(): call(first_kernel, 'first', (jax.ShapeDtypeStruct((tiles // 2, K * BLK, 2...  3.3 us
    pallas_call x2, Pallas kernels, local(): call(next_kernel, 'next', (floats(rows), *outs), [VMEM] * 4 + [ANY] + [VM...  3.08 us

profile of v7, /device:TPU:1, one launch (start us, length us, event | category | flops | bytes accessed | tf_op | source)
XLA Modules:
  0.0 116.3 jit_solution(10775400327166727596)
XLA Ops:
  0.6 0.0 copy-start.1
  0.6 0.0 copy-start
  0.7 0.0 copy-start.2
  1.3 3.3 %first.1 = (f8e4m3fn[8,512,256]{2,1,0:T(32,128)(4,1)S(1)}, f32[16,128]{1,0:T(8,128)S(1)}, f32[8,128]{1,0:T(8,128)S(1)}, f32[512,128]{1,0:T(8,128)S(1)}, f32[8,128]{1,0:T(8,128)S(1)}, /*index=5*/f32[8,128]{1,0:T(8,128)S(1)}) custom-call(s32[4,16]{1,0:T(4,128)} %bitcast.31, s32[16,4,128,128]{3,2,1,0:T(8,128)} %inc_hbm.1, s32[16,128]{1,0:T(8,128)} %cost_ref.3, ...), custom_call_target="tpu_custom_call" | custom-call | tf_op jit(solution)/shard_map/first/pallas_call | solution.py:232
  4.7 15.0 %all_to_all.69.in_ref = f32[32,16,128]{2,1,0:T(8,128)S(1)} all-to-all(f32[32,16,128]{2,1,0:T(8,128)S(1)} %bitcast.30), channel_id=1, replica_groups={{80,104,216,240,168,56,8,192,152,88,48,32,64,160,232,144,112,72,248,208..., dimensions={0} | all-to-all | bytes 524288 | tf_op jit(solution)/shard_map/all_to_all | solution.py:249
  19.7 12.9 %all_to_all.70 = f32[8,1,2176]{2,1,0:T(1,128)S(1)} all-to-all(f32[8,1,2176]{2,1,0:T(1,128)S(1)} %bitcast.22), channel_id=1, replica_groups={{38,0,3,2,37,1,36,39},{46,8,11,10,45,9,44,47},{54,16,19,18,53,17,52,55}..., dimensions={0} | all-to-all | bytes 139264 | tf_op jit(solution)/shard_map/all_to_all | solution.py:220
  32.6 12.2 %all_to_all.71 = f32[32,1,2176]{2,1,0:T(1,128)S(1)} all-to-all(f32[32,1,2176]{2,1,0:T(1,128)S(1)} %bitcast.19), channel_id=1, replica_groups={{80,104,216,240,168,56,8,192,152,88,48,32,64,160,232,144,112,72,248,208..., dimensions={0} | all-to-all | bytes 557056 | tf_op jit(solution)/shard_map/all_to_all | solution.py:220
  44.8 0.0 copy-done.1
  44.8 0.0 copy-done
  44.8 0.0 copy-done.2
  44.8 1.5 %next.2 = (f32[512,128]{1,0:T(8,128)S(1)}, f32[16,128]{1,0:T(8,128)S(1)}, f32[8,128]{1,0:T(8,128)S(1)}, f32[512,128]{1,0:T(8,128)S(1)}, f32[8,128]{1,0:T(8,128)S(1)}) custom-call(f32[544,128]{1,0:T(8,128)S(1)} %bitcast.17, f32[512,128]{1,0:T(8,128)S(1)} %copy-done, f32[8,128]{1,0:T(8,128)S(1)} %get-tuple-element.20.sum_ref, ...), custom_call_target="tpu_custom_call" | custom-call | tf_op jit(solution)/shard_map/next/pallas_call | solution.py:257
  46.3 11.8 %all_to_all.72.in_ref = f32[32,16,128]{2,1,0:T(8,128)S(1)} all-to-all(f32[32,16,128]{2,1,0:T(8,128)S(1)} %bitcast.29), channel_id=1, replica_groups={{80,104,216,240,168,56,8,192,152,88,48,32,64,160,232,144,112,72,248,208..., dimensions={0} | all-to-all | bytes 524288 | tf_op jit(solution)/shard_map/all_to_all | solution.py:249
  58.2 9.6 %all_to_all.73 = f32[8,1,2176]{2,1,0:T(1,128)S(1)} all-to-all(f32[8,1,2176]{2,1,0:T(1,128)S(1)} %bitcast.23), channel_id=1, replica_groups={{38,0,3,2,37,1,36,39},{46,8,11,10,45,9,44,47},{54,16,19,18,53,17,52,55}..., dimensions={0} | all-to-all | bytes 139264 | tf_op jit(solution)/shard_map/all_to_all | solution.py:220
  67.9 12.1 %all_to_all.74 = f32[32,1,2176]{2,1,0:T(1,128)S(1)} all-to-all(f32[32,1,2176]{2,1,0:T(1,128)S(1)} %bitcast.20), channel_id=1, replica_groups={{80,104,216,240,168,56,8,192,152,88,48,32,64,160,232,144,112,72,248,208..., dimensions={0} | all-to-all | bytes 557056 | tf_op jit(solution)/shard_map/all_to_all | solution.py:220
  80.0 1.5 %next.3 = (f32[512,128]{1,0:T(8,128)S(1)}, f32[16,128]{1,0:T(8,128)S(1)}, f32[8,128]{1,0:T(8,128)S(1)}, f32[512,128]{1,0:T(8,128)S(1)}, f32[8,128]{1,0:T(8,128)S(1)}) custom-call(f32[544,128]{1,0:T(8,128)S(1)} %bitcast.16, f32[512,128]{1,0:T(8,128)S(1)} %get-tuple-element.26.mult_ref, f32[8,128]{1,0:T(8,128)S(1)} %get-tuple-element.27.sum_ref, ...), custom_call_target="tpu_custom_call" | custom-call | tf_op jit(solution)/shard_map/next/pallas_call | solution.py:257
  81.6 11.8 %all_to_all.75.in_ref = f32[32,16,128]{2,1,0:T(8,128)S(1)} all-to-all(f32[32,16,128]{2,1,0:T(8,128)S(1)} %bitcast.28), channel_id=1, replica_groups={{80,104,216,240,168,56,8,192,152,88,48,32,64,160,232,144,112,72,248,208..., dimensions={0} | all-to-all | bytes 524288 | tf_op jit(solution)/shard_map/all_to_all | solution.py:249
  93.5 9.4 %all_to_all.76 = f32[8,1,2176]{2,1,0:T(1,128)S(1)} all-to-all(f32[8,1,2176]{2,1,0:T(1,128)S(1)} %bitcast.24), channel_id=1, replica_groups={{38,0,3,2,37,1,36,39},{46,8,11,10,45,9,44,47},{54,16,19,18,53,17,52,55}..., dimensions={0} | all-to-all | bytes 139264 | tf_op jit(solution)/shard_map/all_to_all | solution.py:220
  102.9 12.4 %all_to_all.77 = f32[32,1,2176]{2,1,0:T(1,128)S(1)} all-to-all(f32[32,1,2176]{2,1,0:T(1,128)S(1)} %bitcast.21), channel_id=1, replica_groups={{80,104,216,240,168,56,8,192,152,88,48,32,64,160,232,144,112,72,248,208..., dimensions={0} | all-to-all | bytes 557056 | tf_op jit(solution)/shard_map/all_to_all | solution.py:220
  115.4 0.9 last.1
  (6 shorter events, 0.2 us)
Async XLA Ops:
  0.6 44.2 %copy-start.1 = (s32[16,128]{1,0:T(8,128)S(1)}, s32[16,128]{1,0:T(8,128)}, u32[]{:S(2)}) copy-start(s32[16,128]{1,0:T(8,128)} %cost_ref.3) | copy-start | bytes 24580
  0.6 44.2 %copy-start = (f32[512,128]{1,0:T(8,128)S(1)}, f32[512,128]{1,0:T(8,128)}, u32[]{:S(2)}) copy-start(f32[512,128]{1,0:T(8,128)} %mult_ref.1) | copy-start | bytes 786436
  0.7 44.1 %copy-start.2 = (s32[16,4]{0,1:T(4,128)S(1)}, s32[16,4]{0,1:T(4,128)}, u32[]{:S(2)}) copy-start(s32[16,4]{0,1:T(4,128)} %param.5) | copy-start | bytes 772

commit v8 on v7

--- a/solution.py
+++ b/solution.py
@@ -27,9 +27,9 @@
     return ((x * C + c) * Y + y) * Z + z
 
 
-PLANES = [[device(x, c ^ (z >> 2), y, z) for x, c, y in PLANE_ORDER] for z in range(Z)]
+PLANES = [[device(x, c ^ ((z ^ z >> 2) & 1), y, z) for x, c, y in PLANE_ORDER] for z in range(Z)]
 LINES = [
-    [device(x, c ^ (z >> 2), y, z) for z in LINE_ORDER] for x in range(X) for c in range(C) for y in range(Y)
+    [device(x, c ^ ((z ^ z >> 2) & 1), y, z) for z in LINE_ORDER] for x in range(X) for c in range(C) for y in range(Y)
 ]
 
 f32, bf16 = jnp.float32, jnp.bfloat16
@@ -228,7 +228,7 @@
         return jax.ShapeDtypeStruct((*shape, BLK), f32)
 
     outs = (floats(tiles), floats(8), floats(rows), floats(8))
-    scratch = [pltpu.VMEM((n, BLK), f32) for n in (tiles * K, tiles * 8)]
+    scratch = [pltpu.VMEM((n, BLK), f32) for n in (tiles * K, tiles * 8 + 32)]
     inc, mean, soft, cover, total, top = call(
         first_kernel,
         "first",

time: 117 us -> 117 us (level)
  no operation moved by 1% of the time
where the time goes in v8:
time: 117 us; the launch traced here: 116 us
  blocking collectives  107 us (91%)
  Pallas kernels  7.47 us (6%)
  between operations  1.4 us (1%)
    all_to_all x6, blocking collectives, exchange(): lax.all_to_all(blocks, 'd', 0, 0, tiled=True, axis_index_groups=groups)  68.7 us
    all_to_all x3, blocking collectives, local(): lax.all_to_all(cover.reshape(NEAR, OWN, BLK), 'd', 0, 0, tiled=True, axis...  38.7 us
    pallas_call x1, Pallas kernels, local(): call(first_kernel, 'first', (jax.ShapeDtypeStruct((tiles // 2, K * BLK, 2...  3.3 us
    pallas_call x2, Pallas kernels, local(): call(next_kernel, 'next', (floats(rows), *outs), [VMEM] * 4 + [ANY] + [VM...  3.08 us

profile of v8, /device:TPU:1, one launch (start us, length us, event | category | flops | bytes accessed | tf_op | source)
XLA Modules:
  0.0 116.2 jit_solution(14853995671223847551)
XLA Ops:
  0.6 0.0 copy-start.1
  0.6 0.0 copy-start
  0.7 0.0 copy-start.2
  1.3 3.3 %first.1 = (f8e4m3fn[8,512,256]{2,1,0:T(32,128)(4,1)S(1)}, f32[16,128]{1,0:T(8,128)S(1)}, f32[8,128]{1,0:T(8,128)S(1)}, f32[512,128]{1,0:T(8,128)S(1)}, f32[8,128]{1,0:T(8,128)S(1)}, /*index=5*/f32[8,128]{1,0:T(8,128)S(1)}) custom-call(s32[4,16]{1,0:T(4,128)} %bitcast.31, s32[16,4,128,128]{3,2,1,0:T(8,128)} %inc_hbm.1, s32[16,128]{1,0:T(8,128)} %cost_ref.3, ...), custom_call_target="tpu_custom_call" | custom-call | tf_op jit(solution)/shard_map/first/pallas_call | solution.py:232
  4.7 15.0 %all_to_all.69.in_ref = f32[32,16,128]{2,1,0:T(8,128)S(1)} all-to-all(f32[32,16,128]{2,1,0:T(8,128)S(1)} %bitcast.30), channel_id=1, replica_groups={{80,104,216,240,168,56,8,192,152,88,48,32,64,160,232,144,112,72,248,208..., dimensions={0} | all-to-all | bytes 524288 | tf_op jit(solution)/shard_map/all_to_all | solution.py:249
  19.7 13.2 %all_to_all.70 = f32[8,1,2176]{2,1,0:T(1,128)S(1)} all-to-all(f32[8,1,2176]{2,1,0:T(1,128)S(1)} %bitcast.22), channel_id=1, replica_groups={{38,0,35,2,5,33,36,7},{46,8,43,10,13,41,44,15},{54,16,51,18,21,49,52,23..., dimensions={0} | all-to-all | bytes 139264 | tf_op jit(solution)/shard_map/all_to_all | solution.py:220
  32.9 11.2 %all_to_all.71 = f32[32,1,2176]{2,1,0:T(1,128)S(1)} all-to-all(f32[32,1,2176]{2,1,0:T(1,128)S(1)} %bitcast.19), channel_id=1, replica_groups={{80,104,216,240,168,56,8,192,152,88,48,32,64,160,232,144,112,72,248,208..., dimensions={0} | all-to-all | bytes 557056 | tf_op jit(solution)/shard_map/all_to_all | solution.py:220
  44.2 0.0 copy-done.1
  44.2 0.0 copy-done
  44.2 0.0 copy-done.2
  44.2 1.5 %next.2 = (f32[512,128]{1,0:T(8,128)S(1)}, f32[16,128]{1,0:T(8,128)S(1)}, f32[8,128]{1,0:T(8,128)S(1)}, f32[512,128]{1,0:T(8,128)S(1)}, f32[8,128]{1,0:T(8,128)S(1)}) custom-call(f32[544,128]{1,0:T(8,128)S(1)} %bitcast.17, f32[512,128]{1,0:T(8,128)S(1)} %copy-done, f32[8,128]{1,0:T(8,128)S(1)} %get-tuple-element.20.sum_ref, ...), custom_call_target="tpu_custom_call" | custom-call | tf_op jit(solution)/shard_map/next/pallas_call | solution.py:257
  45.7 11.8 %all_to_all.72.in_ref = f32[32,16,128]{2,1,0:T(8,128)S(1)} all-to-all(f32[32,16,128]{2,1,0:T(8,128)S(1)} %bitcast.29), channel_id=1, replica_groups={{80,104,216,240,168,56,8,192,152,88,48,32,64,160,232,144,112,72,248,208..., dimensions={0} | all-to-all | bytes 524288 | tf_op jit(solution)/shard_map/all_to_all | solution.py:249
  57.6 10.4 %all_to_all.73 = f32[8,1,2176]{2,1,0:T(1,128)S(1)} all-to-all(f32[8,1,2176]{2,1,0:T(1,128)S(1)} %bitcast.23), channel_id=1, replica_groups={{38,0,35,2,5,33,36,7},{46,8,43,10,13,41,44,15},{54,16,51,18,21,49,52,23..., dimensions={0} | all-to-all | bytes 139264 | tf_op jit(solution)/shard_map/all_to_all | solution.py:220
  68.0 11.9 %all_to_all.74 = f32[32,1,2176]{2,1,0:T(1,128)S(1)} all-to-all(f32[32,1,2176]{2,1,0:T(1,128)S(1)} %bitcast.20), channel_id=1, replica_groups={{80,104,216,240,168,56,8,192,152,88,48,32,64,160,232,144,112,72,248,208..., dimensions={0} | all-to-all | bytes 557056 | tf_op jit(solution)/shard_map/all_to_all | solution.py:220
  80.0 1.5 %next.3 = (f32[512,128]{1,0:T(8,128)S(1)}, f32[16,128]{1,0:T(8,128)S(1)}, f32[8,128]{1,0:T(8,128)S(1)}, f32[512,128]{1,0:T(8,128)S(1)}, f32[8,128]{1,0:T(8,128)S(1)}) custom-call(f32[544,128]{1,0:T(8,128)S(1)} %bitcast.16, f32[512,128]{1,0:T(8,128)S(1)} %get-tuple-element.26.mult_ref, f32[8,128]{1,0:T(8,128)S(1)} %get-tuple-element.27.sum_ref, ...), custom_call_target="tpu_custom_call" | custom-call | tf_op jit(solution)/shard_map/next/pallas_call | solution.py:257
  81.5 11.8 %all_to_all.75.in_ref = f32[32,16,128]{2,1,0:T(8,128)S(1)} all-to-all(f32[32,16,128]{2,1,0:T(8,128)S(1)} %bitcast.28), channel_id=1, replica_groups={{80,104,216,240,168,56,8,192,152,88,48,32,64,160,232,144,112,72,248,208..., dimensions={0} | all-to-all | bytes 524288 | tf_op jit(solution)/shard_map/all_to_all | solution.py:249
  93.4 9.8 %all_to_all.76 = f32[8,1,2176]{2,1,0:T(1,128)S(1)} all-to-all(f32[8,1,2176]{2,1,0:T(1,128)S(1)} %bitcast.24), channel_id=1, replica_groups={{38,0,35,2,5,33,36,7},{46,8,43,10,13,41,44,15},{54,16,51,18,21,49,52,23..., dimensions={0} | all-to-all | bytes 139264 | tf_op jit(solution)/shard_map/all_to_all | solution.py:220
  103.2 12.1 %all_to_all.77 = f32[32,1,2176]{2,1,0:T(1,128)S(1)} all-to-all(f32[32,1,2176]{2,1,0:T(1,128)S(1)} %bitcast.21), channel_id=1, replica_groups={{80,104,216,240,168,56,8,192,152,88,48,32,64,160,232,144,112,72,248,208..., dimensions={0} | all-to-all | bytes 557056 | tf_op jit(solution)/shard_map/all_to_all | solution.py:220
  115.3 0.9 last.1
  (6 shorter events, 0.2 us)
Async XLA Ops:
  0.6 43.6 %copy-start.1 = (s32[16,128]{1,0:T(8,128)S(1)}, s32[16,128]{1,0:T(8,128)}, u32[]{:S(2)}) copy-start(s32[16,128]{1,0:T(8,128)} %cost_ref.3) | copy-start | bytes 24580
  0.6 43.6 %copy-start = (f32[512,128]{1,0:T(8,128)S(1)}, f32[512,128]{1,0:T(8,128)}, u32[]{:S(2)}) copy-start(f32[512,128]{1,0:T(8,128)} %mult_ref.1) | copy-start | bytes 786436
  0.7 43.5 %copy-start.2 = (s32[16,4]{0,1:T(4,128)S(1)}, s32[16,4]{0,1:T(4,128)}, u32[]{:S(2)}) copy-start(s32[16,4]{0,1:T(4,128)} %param.5) | copy-start | bytes 772
